TPU v7x, 256 devices: a whole 4x4x8 slice. The times are simulated.
256 devices in a mesh: sample: 16 (over z, y_hi), span: 8 (over x, y_lo), kvhead: 2 (over core).
Axes of the slice: x: 4, y: 4 (y_hi: 2, y_lo: 2; y = y_hi * 2 + y_lo), z: 8, core: 2. Of those that a mesh axis runs over, the one named last changes fastest.
Arguments:
- queries: bfloat16 [16, 256, 3584], P('sample', None, 'kvhead'), may hold values from -6 to 6
- outputs: bfloat16 [16, 256, 3584], P('sample', None, 'kvhead'), may hold values from -6 to 6
- grad_out: bfloat16 [16, 256, 3584], P('sample', None, 'kvhead'), may hold values from -48 to 48
- log_norms: float32 [16, 28, 256], P('sample', 'kvhead'), as said below
- lengths: int32 [16], P('sample'), may hold values from 1 to 256, 1024 in all
- prompt_key_rows: bfloat16 [16384, 512], P(('sample', 'span'), 'kvhead'), may hold values from -9 to 9
- prompt_value_rows: bfloat16 [16384, 512], P(('sample', 'span'), 'kvhead'), may hold values from -6 to 6
- slice_key_rows: bfloat16 [16, 256, 512], P('sample', 'span', 'kvhead'), may hold values from -9 to 9
- slice_value_rows: bfloat16 [16, 256, 512], P('sample', 'span', 'kvhead'), may hold values from -6 to 6
Outputs:
- grad_queries: bfloat16 [16, 256, 3584], P('sample', 'span', 'kvhead')
- grad_k_prompt: bfloat16 [16384, 512], P(('sample', 'span'), 'kvhead')
- grad_v_prompt: bfloat16 [16384, 512], P(('sample', 'span'), 'kvhead')
- grad_k_self: bfloat16 [16, 256, 512], P('sample', 'span', 'kvhead')
- grad_v_self: bfloat16 [16, 256, 512], P('sample', 'span', 'kvhead')
Inputs may be any that keep to these rules, and one draw needn't show every extreme that they name: `log_norms`: every entry lies between 0.8 and 2.4 above the natural logarithm of 16640.
All inputs are finite; a program needn't handle non-finite values. No bound on the sum of `lengths` on one device may be relied on, other than what follows from the above.
Results may differ from a plain program's by a relative error of at most 0.0051.
Values may be sent and summed in bfloat16 or wider, within the bound.
No kernel may reach another device: no remote copies, remote signals or barrier semaphores. Data moves between devices by JAX's collectives and lax.ppermute only.
A program may use at most 64 MiB of HBM per device.

v0:
```python
import math

import jax
import jax.numpy as jnp
from jax import lax
from jax.experimental import pallas as pl
from jax.experimental.pallas import tpu as pltpu
from jax.sharding import Mesh
from jax.sharding import PartitionSpec as P

HEAD_WIDTH = 128
SAMPLE = ("sample_0", "sample_1")
SPAN = ("span_0", "span_1")
SAMPLE_SPAN = SAMPLE + SPAN
ALONG_X, ALONG_Y = "span_0", ("sample_1", "span_1")
GROUP = 7
CLASSES = 8
SLOTS = 24
LIVE = 144
STATS = GROUP * HEAD_WIDTH
INTERPRET = False
VMEM_BYTES = 24 * 1024 * 1024
BF16 = jnp.bfloat16
F32 = jnp.float32
SCALE = 1.0 / math.sqrt(HEAD_WIDTH)


def exchange(tiles, axes):
    return lax.all_to_all(tiles, axes, split_axis=0, concat_axis=0, tiled=True)


def dot(a, b, ca, cb):
    return lax.dot_general(a, b, (((ca,), (cb,)), ((), ())), preferred_element_type=F32)


def call(body, out_shape, *args, **kw):
    params = pltpu.CompilerParams(vmem_limit_bytes=VMEM_BYTES)
    return pl.pallas_call(
        body, out_shape=out_shape, interpret=INTERPRET, compiler_params=params, **kw
    )(*args)


def stat_lanes(shape):
    lane = lax.broadcasted_iota(jnp.int32, shape, 1)
    group = jnp.zeros(shape, jnp.int32)
    for edge in range(GROUP, 6 * GROUP, GROUP):
        group = group + jnp.where(lane >= edge, 1, 0)
    piece = jnp.where(group >= 3, group - 3, group)
    return lane, lane - GROUP * group, piece


def pick_kernel(p_ref, turn_ref, live_ref, q_ref, o_ref, g_ref, norm_ref, out_ref):
    p, turn, live = p_ref[0], turn_ref[0], live_ref[0]
    row = lax.broadcasted_iota(jnp.int32, (64, 256), 0)
    i = lax.broadcasted_iota(jnp.int32, (64, 256), 1)
    hit = (i % 8 == p) & (i < live) & ((turn + i // 8) % 8 == row // 8) & (i // 64 == row % 4)
    pick_q = jnp.where(hit & (row % 8 < 4), 1.0, 0.0)
    pick_g = jnp.where(hit & (row % 8 >= 4), 1.0, 0.0).astype(BF16)
    lane, head_of, piece = stat_lanes((64, HEAD_WIDTH))
    pick_q_low = pick_q.astype(BF16)
    for half in range(2):
        lanes = slice(half * STATS, (half + 1) * STATS)
        both = dot(pick_q_low, q_ref[:, lanes], 1, 0) + dot(pick_g, g_ref[:, lanes], 1, 0)
        out_ref[:, half, :, 0:STATS] = both.reshape(8, 8, STATS).astype(BF16)
        product = dot(pick_q_low, o_ref[:, lanes], 1, 0) * dot(pick_q_low, g_ref[:, lanes], 1, 0)
        stat = jnp.zeros((64, HEAD_WIDTH), F32)
        for inner in range(GROUP):
            mine = head_of == inner
            part = product[:, inner * HEAD_WIDTH : (inner + 1) * HEAD_WIDTH]
            delta = jnp.sum(part, axis=1, keepdims=True)
            norm = norm_ref[half * GROUP + inner]
            norm = jnp.sum(pick_q * norm, axis=1, keepdims=True) * math.sqrt(HEAD_WIDTH)
            stat = jnp.where(mine & (lane < 3 * GROUP), norm, stat)
            stat = jnp.where(mine & (lane >= 3 * GROUP) & (lane < 6 * GROUP), delta, stat)
        high = stat.astype(BF16).astype(F32)
        middle = (stat - high).astype(BF16).astype(F32)
        low = stat - high - middle
        stat = jnp.where(piece == 0, high, jnp.where(piece == 1, middle, low))
        stat = jnp.where(lane == 6 * GROUP, live.astype(F32), stat)
        out_ref[:, half, :, STATS:] = stat.reshape(8, 8, HEAD_WIDTH).astype(BF16)


def compact_kernel(p_ref, z_ref, rows_ref, out_ref):
    rows = rows_ref[...].reshape(128, 1024)
    shape = (128, 128)
    row = lax.broadcasted_iota(jnp.int32, shape, 0)
    col = lax.broadcasted_iota(jnp.int32, shape, 1)
    length = rows[:, STATS + 6 * GROUP : STATS + 6 * GROUP + 1].astype(F32)
    length = jnp.broadcast_to(length, shape).astype(jnp.int32)
    count = (length - p_ref[0] + 7) >> 3
    valid = 8 * (row & 3) + ((z_ref[0] - (row >> 3)) & 7) < count
    earlier = jnp.where(((col >> 3) < (row >> 3)) & (((col >> 2) & 1) == 0), 1.0, 0.0)
    before = dot(earlier.astype(BF16), jnp.where(valid, 1.0, 0.0).astype(BF16), 1, 0)
    place = before.astype(jnp.int32) + (row & 3) + SLOTS * ((row >> 2) & 1)
    pick = jnp.where(valid & (place == col), 1.0, 0.0).astype(BF16)
    rows = dot(pick, rows, 0, 0)[0 : 2 * SLOTS].astype(BF16)
    for copy in range(out_ref.shape[0]):
        out_ref[copy] = rows


def prompt_kernel(in_slot_ref, out_slot_ref, rows_ref, *refs):
    kv_refs, kvg_refs = refs[0:4], refs[4:8]
    gq_ref, q_scr, g_scr, acc_ref, back_ref = refs[8:]
    acc_ref[...] = jnp.zeros_like(acc_ref)
    slot = in_slot_ref[0:1, :]
    hit = lax.broadcasted_iota(jnp.int32, (2 * LIVE, slot.shape[1]), 0) == slot
    pick = jnp.where(hit, 1.0, 0.0).astype(BF16)
    rows = dot(pick, rows_ref[...].reshape(slot.shape[1], -1), 1, 0).astype(BF16)
    lane, head_of, _ = stat_lanes((LIVE, HEAD_WIDTH))
    stats = rows[0:LIVE, STATS:]
    zero = jnp.zeros((), BF16)
    for head in range(GROUP):
        place = slice(head * LIVE, (head + 1) * LIVE)
        lanes = slice(head * HEAD_WIDTH, (head + 1) * HEAD_WIDTH)
        mine = head_of == head
        q_scr[place, 0:HEAD_WIDTH] = rows[0:LIVE, lanes]
        q_scr[place, HEAD_WIDTH:] = jnp.where(mine & (lane < 3 * GROUP), stats, zero)
        g_scr[place, 0:HEAD_WIDTH] = rows[LIVE:, lanes]
        g_scr[place, HEAD_WIDTH:] = jnp.where(
            mine & (lane >= 3 * GROUP) & (lane < 6 * GROUP), stats, zero
        )
    q_scr[GROUP * LIVE :, :] = jnp.zeros((1024 - GROUP * LIVE, 2 * HEAD_WIDTH), BF16)
    g_scr[GROUP * LIVE :, :] = jnp.zeros((1024 - GROUP * LIVE, 2 * HEAD_WIDTH), BF16)

    lane = lax.broadcasted_iota(jnp.int32, (256, HEAD_WIDTH), 1)
    minus = jnp.where(lane < 6 * GROUP, -1.0, 0.0).astype(BF16)

    def block(kv_ref, kvg_ref, pair):
        def piece(k):
            return pl.ds(pl.multiple_of(pair * 512 + k * 128, 128), 128)

        keys = jnp.concatenate([kv_ref[piece(0), :], kv_ref[piece(2), :]], axis=0)
        values = jnp.concatenate([kv_ref[piece(1), :], kv_ref[piece(3), :]], axis=0)
        wide_keys = jnp.concatenate([keys, minus], axis=1)
        wide_values = jnp.concatenate([values, minus], axis=1)
        gk = jnp.zeros(keys.shape, F32)
        gv = jnp.zeros(keys.shape, F32)
        for part in range(4):
            rows = slice(256 * part, 256 * part + 256)
            prob = jnp.exp(dot(wide_keys, q_scr[rows, :], 1, 1) * SCALE)
            sgrad = (prob * dot(wide_values, g_scr[rows, :], 1, 1)).astype(BF16)
            gv = gv + dot(prob.astype(BF16), g_scr[rows, 0:HEAD_WIDTH], 1, 0)
            gk = gk + dot(sgrad, q_scr[rows, 0:HEAD_WIDTH], 1, 0)
            acc_ref[rows, :] += dot(sgrad, keys, 0, 0)
        gk, gv = (gk * SCALE).astype(BF16), gv.astype(BF16)
        for k, part in enumerate((gk[0:128], gv[0:128], gk[128:256], gv[128:256])):
            kvg_ref[piece(k), :] = part

    for kv_ref, kvg_ref in zip(kv_refs, kvg_refs):
        lax.fori_loop(0, 2, lambda k, _: block(kv_ref, kvg_ref, k), None)

    back_ref[...] = jnp.zeros_like(back_ref)
    for head in range(GROUP):
        lanes = slice(head % 4 * HEAD_WIDTH, (head % 4 + 1) * HEAD_WIDTH)
        part = (acc_ref[head * LIVE : (head + 1) * LIVE, :] * SCALE).astype(BF16)
        back_ref[head // 4 * LIVE : (head // 4 + 1) * LIVE, lanes] = part
    slot = out_slot_ref[0:1, :]
    hit = lax.broadcasted_iota(jnp.int32, (2 * LIVE, slot.shape[1]), 0) == slot
    pick = jnp.where(hit, 1.0, 0.0).astype(BF16)
    gq_ref[...] = dot(pick, back_ref[...], 0, 0).reshape(gq_ref.shape).astype(BF16)


def prompt_terms(in_slot, out_slot, rows, *kv):
    *kv_grads, gq = call(
        prompt_kernel,
        [jax.ShapeDtypeStruct((1024, HEAD_WIDTH), BF16)] * 4
        + [jax.ShapeDtypeStruct((128, 8, 512), BF16)],
        in_slot,
        out_slot,
        rows,
        *kv,
        scratch_shapes=[
            pltpu.VMEM((1024, 2 * HEAD_WIDTH), BF16),
            pltpu.VMEM((1024, 2 * HEAD_WIDTH), BF16),
            pltpu.VMEM((1024, HEAD_WIDTH), F32),
            pltpu.VMEM((2 * LIVE, 512), BF16),
        ],
    )
    return kv_grads, gq


def final_kernel(parts_ref, own_ref, out_ref, sum_ref):
    for half in range(2):
        for p in range(CLASSES):
            total = parts_ref[half * 8 + p].astype(F32)
            for z in range(1, 8):
                total = total + parts_ref[z * 16 + half * 8 + p].astype(F32)
            for head in range(GROUP):
                rows = slice(head // 4 * 4, head // 4 * 4 + 4)
                part = total[rows, head % 4 * HEAD_WIDTH : (head % 4 + 1) * HEAD_WIDTH]
                first = (half * GROUP + head) * 32 + p
                sum_ref[pl.ds(first, 4, stride=8), :] = part
    for head in range(2 * GROUP):
        lanes = slice(head * HEAD_WIDTH, (head + 1) * HEAD_WIDTH)
        out_ref[:, lanes] = (sum_ref[head * 32 : head * 32 + 32, :] + own_ref[:, lanes]).astype(BF16)


def pack_kernel(info, pk_ref, pv_ref, sk_ref, sv_ref, own_ref, other_ref):
    half = info[0]
    low, high = slice(0, HEAD_WIDTH), slice(HEAD_WIDTH, 2 * HEAD_WIDTH)
    for k, ref in enumerate((pk_ref, pv_ref)):
        rows = slice(128 * k, 128 * k + 128)
        own_ref[rows, :] = jnp.where(half == 0, ref[:, low], ref[:, high])
        other_ref[rows, :] = jnp.where(half == 0, ref[:, high], ref[:, low])
    for k, (ref, lanes) in enumerate(((sk_ref, low), (sk_ref, high), (sv_ref, low), (sv_ref, high))):
        own_ref[256 + 32 * k : 288 + 32 * k, :] = ref[:, lanes]


def x_sum_kernel(a_ref, b_ref, c_ref, d_ref, *out_refs):
    for k, out_ref in enumerate(out_refs):
        rows = slice(256 * k, 256 * k + 256)
        total = a_ref[rows, :].astype(F32) + b_ref[rows, :].astype(F32)
        total = total + c_ref[rows, :].astype(F32) + d_ref[rows, :].astype(F32)
        out_ref[...] = total.astype(BF16)


def y_sum_kernel(info, a_ref, b_ref, c_ref, d_ref, k_ref, v_ref):
    half = info[0]
    own = a_ref[...].astype(F32) + b_ref[...].astype(F32)
    other = c_ref[...].astype(F32) + d_ref[...].astype(F32)
    low = jnp.where(half == 0, own, other).astype(BF16)
    high = jnp.where(half == 0, other, own).astype(BF16)
    for k, ref in enumerate((k_ref, v_ref)):
        ref[:, 0:HEAD_WIDTH] = low[128 * k : 128 * k + 128]
        ref[:, HEAD_WIDTH:] = high[128 * k : 128 * k + 128]


def shifted(value, by):
    return lax.ppermute(value, ALONG_X, [(k, (k + by) % 4) for k in range(4)])


def crossed(value, by):
    return lax.ppermute(value, ALONG_Y, [(k, k ^ by) for k in range(4)])


def self_kernel(
    p_ref, live_ref, q_ref, g_ref, norm_ref, delta_ref, col_norm_ref, col_delta_ref, kv0_ref, kv1_ref, kv2_ref,
    kv3_ref, gk_ref, gv_ref, gq_ref,
):
    p, live = p_ref[0], live_ref[0]
    rows_total = q_ref.shape[0]
    i_row = lax.broadcasted_iota(jnp.int32, (32, rows_total), 1)
    j_row = lax.broadcasted_iota(jnp.int32, (32, rows_total), 0) + p * 32
    live_row = lax.broadcasted_iota(jnp.int32, (rows_total, HEAD_WIDTH), 0) < live
    live_own = lax.broadcasted_iota(jnp.int32, (32, HEAD_WIDTH), 0) + p * 32 < live
    zero = jnp.zeros((), BF16)
    kv_refs = (kv0_ref, kv1_ref, kv2_ref, kv3_ref)
    lane = lax.broadcasted_iota(jnp.int32, (1, rows_total), 1)
    block = lane // 32
    from_span = (p // 2 + 4 - block // 2) % 4 * 2 + (p % 2 + block % 2) % 2
    position = from_span * 32 + lane % 32
    for kv in range(2):
        key_lanes = slice(kv * HEAD_WIDTH, (kv + 1) * HEAD_WIDTH)

        def piece(ref, which, kind):
            first = 1024 + 128 * which + 32 * (2 * kind + kv)
            return ref[first : first + 32, :]

        keys, values = piece(kv0_ref, 0, 0), piece(kv0_ref, 0, 1)
        all_keys = jnp.concatenate([piece(r, w, 0) for r in kv_refs for w in range(2)], axis=0)
        all_values = jnp.concatenate([piece(r, w, 1) for r in kv_refs for w in range(2)], axis=0)
        gk = jnp.zeros((32, HEAD_WIDTH), F32)
        gv = jnp.zeros((32, HEAD_WIDTH), F32)
        for inner in range(GROUP):
            head = kv * GROUP + inner
            lanes = slice(head * HEAD_WIDTH, (head + 1) * HEAD_WIDTH)
            q = q_ref[:, lanes]
            g = jnp.where(live_row, g_ref[:, lanes], zero)
            prob = jnp.exp(dot(keys, q, 1, 1) * SCALE - norm_ref[head])
            prob = jnp.where(j_row <= i_row, prob, 0.0)
            sgrad = prob * (dot(values, g, 1, 1) - delta_ref[head : head + 1, :])
            gv = gv + dot(prob.astype(BF16), g, 1, 0)
            gk = gk + dot(sgrad.astype(BF16), q, 1, 0)
            q_own = q_ref[pl.ds(pl.multiple_of(p * 32, 32), 32), lanes]
            g_own = g_ref[pl.ds(pl.multiple_of(p * 32, 32), 32), lanes]
            g_own = jnp.where(live_own, g_own, zero)
            prob = jnp.exp(dot(q_own, all_keys, 1, 1) * SCALE - col_norm_ref[:, head : head + 1])
            i_own = lax.broadcasted_iota(jnp.int32, prob.shape, 0) + p * 32
            prob = jnp.where(position <= i_own, prob, 0.0)
            sgrad = prob * (dot(g_own, all_values, 1, 1) - col_delta_ref[:, head : head + 1])
            gq_ref[:, lanes] = dot(sgrad.astype(BF16), all_keys, 1, 0) * SCALE
        gk_ref[:, key_lanes] = (gk * SCALE).astype(BF16)
        gv_ref[:, key_lanes] = gv.astype(BF16)


def shards(
    queries,
    outputs,
    grad_out,
    log_norms,
    lengths,
    prompt_key_rows,
    prompt_value_rows,
    slice_key_rows,
    slice_value_rows,
):
    z = lax.axis_index("sample_0")
    half = lax.axis_index("sample_1")
    p = lax.axis_index(SPAN)
    sample = 2 * z + half
    spans = lax.axis_size(SPAN)
    slice_rows = queries.shape[1]
    heads = queries.shape[2] // HEAD_WIDTH
    class_rows = slice_rows // CLASSES
    q, o, g = queries[0], outputs[0], grad_out[0]
    norms = log_norms.transpose(1, 0, 2)
    live = lengths[0]
    smem, vmem = pl.BlockSpec(memory_space=pltpu.SMEM), pl.BlockSpec(memory_space=pltpu.VMEM)

    picked = call(
        pick_kernel,
        jax.ShapeDtypeStruct((8, 2, 8, 1024), BF16),
        p[None],
        (sample % 8)[None],
        lengths,
        q,
        o,
        g,
        norms,
        in_specs=[smem] * 3 + [vmem] * 4,
    )
    arrived = exchange(picked.reshape(16, 8, 1024), SAMPLE)

    packed = lambda rows: jax.ShapeDtypeStruct((rows, HEAD_WIDTH), BF16)
    own, other = call(
        pack_kernel,
        [packed(384), packed(256)],
        half[None],
        prompt_key_rows,
        prompt_value_rows,
        slice_key_rows[0],
        slice_value_rows[0],
        in_specs=[smem] + [vmem] * 4,
    )
    beside = crossed(own, 1)
    column = jnp.concatenate(
        [own[:256], beside[:256], crossed(other, 2), crossed(other, 3), own[256:], beside[256:]]
    )
    kv = [column] + [shifted(column, k) for k in (1, 2, 3)]

    all_lengths = arrived[:, 0, STATS + 6 * GROUP].astype(jnp.int32)
    live_of = jnp.clip((all_lengths - p + CLASSES - 1) // CLASSES, 0, class_rows)
    every_sample = jnp.arange(16)
    first = (jnp.arange(8)[None, :] - every_sample[:, None]) % 8
    held = jnp.clip((live_of[:, None] - first + 7) // 8, 0, 4)
    earlier = (every_sample[None, :] < every_sample[:, None])[:, :, None]
    before = jnp.sum(jnp.where(earlier, held[None], 0), axis=1)
    total = jnp.sum(held, axis=0)
    base = jnp.sum(jnp.where(jnp.arange(8)[None, :] < jnp.arange(8)[:, None], total[None], 0), axis=1)
    compact = call(
        compact_kernel,
        jax.ShapeDtypeStruct((8, 2 * SLOTS, 1024), BF16),
        p[None],
        z[None],
        arrived,
        in_specs=[smem, smem, vmem],
    )
    rows = exchange(compact, "sample_0")
    step = jnp.arange(SLOTS)[None, :]
    in_slot = base[:, None] + step
    in_slot = in_slot[:, None, :] + LIVE * jnp.arange(2)[None, :, None]
    in_slot = jnp.where((step < total[:, None])[:, None, :], in_slot, -1).reshape(1, 16 * SLOTS)
    k = jnp.arange(class_rows)
    holder = (k[None, :] + every_sample[:, None]) % 8
    chosen = holder[:, :, None] == jnp.arange(8)[None, None, :]
    slot_of = jnp.sum(jnp.where(chosen, (base[None, :] + before)[:, None, :], 0), axis=2)
    slot_of = jnp.where(k[None, :] < live_of[:, None], slot_of + k[None, :] // 8, -LIVE * 2)
    out_slot = slot_of.reshape(16, spans, 1, 4) + LIVE * jnp.arange(2)[None, None, :, None]
    out_slot = out_slot.reshape(1, 1024)

    live_rows = lax.broadcasted_iota(jnp.int32, (slice_rows, 1), 0) < live
    g_live = jnp.where(live_rows, g, jnp.zeros((), BF16))
    delta = jnp.sum(
        (g_live.astype(F32) * o.astype(F32)).reshape(slice_rows, heads, HEAD_WIDTH), axis=-1
    ).T
    own_rows = slice_rows // spans
    col_norms = lax.dynamic_slice_in_dim(log_norms[0], p * own_rows, own_rows, 1).T
    col_delta = lax.dynamic_slice_in_dim(delta, p * own_rows, own_rows, 1).T
    rows, delta, col_norms, col_delta = lax.optimization_barrier(
        (rows, delta, col_norms, col_delta)
    )
    own_shape = jax.ShapeDtypeStruct((own_rows, 2 * HEAD_WIDTH), BF16)
    gk_self, gv_self, gq_self = call(
        self_kernel,
        [own_shape, own_shape, jax.ShapeDtypeStruct((own_rows, heads * HEAD_WIDTH), F32)],
        p[None],
        lengths,
        q,
        g,
        norms,
        delta,
        col_norms,
        col_delta,
        *kv,
        in_specs=[smem] * 2 + [vmem] * 10,
    )

    kv_grads, gq_parts = prompt_terms(in_slot, out_slot, rows, *kv)
    gq_parts = exchange(gq_parts, SAMPLE_SPAN)
    parts = [kv_grads[0]] + [shifted(kv_grads[k], -k) for k in (1, 2, 3)]
    *parts, gq_self = lax.optimization_barrier((*parts, gq_self))
    parts = call(x_sum_kernel, [packed(256)] * 4, *parts)
    parts = [parts[0]] + [crossed(parts[k], k) for k in (1, 2, 3)]
    prompt_shape = jax.ShapeDtypeStruct(prompt_key_rows.shape, BF16)
    gk_prompt, gv_prompt = call(
        y_sum_kernel,
        [prompt_shape, prompt_shape],
        half[None],
        *parts,
        in_specs=[smem] + [vmem] * 4,
    )
    grad_query = call(
        final_kernel,
        jax.ShapeDtypeStruct((own_rows, heads * HEAD_WIDTH), BF16),
        gq_parts,
        gq_self,
        scratch_shapes=[pltpu.VMEM((heads * own_rows, HEAD_WIDTH), F32)],
    )
    return grad_query[None], gk_prompt, gv_prompt, gk_self[None], gv_self[None]


def solution(mesh):
    split = Mesh(
        mesh.devices.reshape(8, 2, 4, 2, mesh.shape["kvhead"]), SAMPLE_SPAN + ("kvhead",)
    )
    placed = (
        P(SAMPLE, None, "kvhead"),
        P(SAMPLE, None, "kvhead"),
        P(SAMPLE, None, "kvhead"),
        P(SAMPLE, "kvhead", None),
        P(SAMPLE),
        P(SAMPLE_SPAN, "kvhead"),
        P(SAMPLE_SPAN, "kvhead"),
        P(SAMPLE, SPAN, "kvhead"),
        P(SAMPLE, SPAN, "kvhead"),
    )

    return jax.shard_map(
        shards,
        mesh=split,
        in_specs=placed,
        out_specs=(
            P(SAMPLE, SPAN, "kvhead"),
            P(SAMPLE_SPAN, "kvhead"),
            P(SAMPLE_SPAN, "kvhead"),
            P(SAMPLE, SPAN, "kvhead"),
            P(SAMPLE, SPAN, "kvhead"),
        ),
        check_vma=False,
    )
```

profile of v0, /device:TPU:1, one launch (start us, length us, event | category | flops | bytes accessed | tf_op | source)
XLA Modules:
  0.0 126.8 jit_solution(14396706241459552156)
XLA Ops:
  0.6 0.8 copy-done.20
  1.5 0.8 copy-done.21
  2.3 0.7 copy-done.22
  3.0 0.7 copy-done.23
  3.8 3.6 %collective-permute-start.2 = (bf16[256,128]{1,0:T(8,128)(2,1)S(1)}, bf16[256,128]{1,0:T(8,128)(2,1)S(1)}, u32[]{:S(2)}, u32[]{:S(2)}) collective-permute-start(bf16[256,128]{1,0:T(8,128)(2,1)S(1)} %get-tuple-element.32), channel_id=1, source_target_pairs={{0,18},{2,16},{16,2},{18,0},{1,19},{3,17},{17,3},{19,1},{4,22},{6,... | collective-permute-start | bytes 196616 | tf_op jit(solution)/shard_map/ppermute | solution.py:233
  8.8 1.2 copy-done
  9.9 1.2 copy-done.2
  11.1 1.2 copy-done.4
  12.3 0.7 copy-done.15
  13.0 1.5 %shard_map.128 = bf16[8,2,8,1024]{3,2,1,0:T(8,128)(2,1)} custom-call(s32[1]{0:T(128)} %bitcast.p_ref, s32[1]{0:T(128)} %bitcast.1.turn_ref, s32[1]{0:T(128)} %copy.38.live_ref, bf16[256,1792]{1,0:T(8,128)(2,1)S(1)} %bitcast.27, bf16[256,1792]{1,0:T(8,128)(2,1)S(1)} %bitcast.26, bf16[256,1792]{1,0:T(8,128)(2,1)S(1)} %bitcast.24, f32[14,1,256]{2,1,0:T(1,128)S(1)} %bitcast.30), custom_call_target="tpu_custom_call" | custom-call | tf_op jit(solution)/shard_map/pallas_call | solution.py:38
  14.5 10.8 %all-to-all-start = ((bf16[16,8,1024]{2,1,0:T(8,128)(2,1)}), bf16[16,8,1024]{2,1,0:T(8,128)(2,1)S(1)}, u32[]{:S(2)}, u32[]{:S(2)}) async-start(bf16[16,8,1024]{2,1,0:T(8,128)(2,1)} %bitcast.6), calls=%async_computation | async-start | bytes 524288 | tf_op jit(solution)/shard_map/all_to_all | solution.py:29
  25.3 1.3 %copy.29 = bf16[1,256,1792]{1,2,0:T(8,128)(2,1)} copy(bf16[1,256,1792]{2,1,0:T(8,128)(2,1)S(1)} %copy-done.3) | data formatting | bytes 1835008 | tf_op args[1]
  26.7 1.3 %copy.28 = bf16[1,256,1792]{1,2,0:T(8,128)(2,1)} copy(bf16[1,256,1792]{2,1,0:T(8,128)(2,1)S(1)} %copy-done.1) | data formatting | bytes 1835008 | tf_op args[2]
  28.1 0.7 copy.30
  28.8 1.5 %fusion = f32[256,14]{0,1:T(8,128)S(1)} fusion(bf16[256,14,128]{0,2,1:T(8,128)(2,1)S(1)} %bitcast.35, bf16[256,14,128]{0,2,1:T(8,128)(2,1)} %bitcast.36, pred[256]{0:T(512)(128)(4,1)S(1)} %iota_compare_fusion.4), kind=kLoop, calls=%fused_computation.1 | loop fusion | flops 2290176 | bytes 1849600 | tf_op jit(solution)/shard_map/reduce_sum | solution.py:373
  30.4 0.7 copy.32.col_delta_ref
  31.2 2.6 %collective-permute-start.5 = (bf16[1280,128]{1,0:T(8,128)(2,1)S(1)}, bf16[1280,128]{1,0:T(8,128)(2,1)S(1)}, u32[]{:S(2)}, u32[]{:S(2)}) collective-permute-start(bf16[1280,128]{1,0:T(8,128)(2,1)S(1)} %slice_dynamic-update-slice_fusion.2.refs_0_.kv0_ref), channel_id=1, source_target_pairs={{0,12},{4,0},{8,4},{12,8},{1,13},{5,1},{9,5},{13,9},{2,14},{6,2},{... | collective-permute-start | bytes 983048 | tf_op jit(solution)/shard_map/ppermute | solution.py:229
  34.3 0.6 collective-permute-start.3
  34.9 1.6 %all-to-all-done.rows_ref = bf16[16,8,1024]{2,1,0:T(8,128)(2,1)S(1)} async-done(((bf16[16,8,1024]{2,1,0:T(8,128)(2,1)}), bf16[16,8,1024]{2,1,0:T(8,128)(2,1)S(1)}, u32[]{:S(2)}, u32[]{:S(2)}) %all-to-all-start) | async-done | bytes 262176 | tf_op jit(solution)/shard_map/all_to_all | solution.py:29
  37.2 1.4 %shard_map.129 = bf16[8,48,1024]{2,1,0:T(8,128)(2,1)} custom-call(s32[1]{0:T(128)} %bitcast.p_ref, s32[1]{0:T(128)} %bitcast.8.z_ref, bf16[16,8,1024]{2,1,0:T(8,128)(2,1)S(1)} %all-to-all-done.rows_ref), custom_call_target="tpu_custom_call" | custom-call | tf_op jit(solution)/shard_map/pallas_call | solution.py:38
  38.7 4.9 %all-to-all-start.1 = ((bf16[8,48,1024]{2,1,0:T(8,128)(2,1)}), bf16[8,48,1024]{2,1,0:T(8,128)(2,1)S(1)}, u32[]{:S(2)}, u32[]{:S(2)}) async-start(bf16[8,48,1024]{2,1,0:T(8,128)(2,1)} %shard_map.129), calls=%async_computation.1 | async-start | bytes 1572864 | tf_op jit(solution)/shard_map/all_to_all | solution.py:29
  44.7 0.8 broadcast_add_fusion
  45.7 18.5 %all-to-all-done.1.rows_ref = bf16[8,48,1024]{2,1,0:T(8,128)(2,1)S(1)} async-done(((bf16[8,48,1024]{2,1,0:T(8,128)(2,1)}), bf16[8,48,1024]{2,1,0:T(8,128)(2,1)S(1)}, u32[]{:S(2)}, u32[]{:S(2)}) %all-to-all-start.1) | async-done | bytes 786464 | tf_op jit(solution)/shard_map/all_to_all | solution.py:29
  64.2 12.3 %shard_map.131 = (bf16[1024,128]{1,0:T(8,128)(2,1)S(1)}, bf16[1024,128]{1,0:T(8,128)(2,1)S(1)}, bf16[1024,128]{1,0:T(8,128)(2,1)S(1)}, bf16[1024,128]{1,0:T(8,128)(2,1)S(1)}, bf16[128,8,512]{2,1,0:T(8,128)(2,1)S(1)}) custom-call(s32[1,384]{1,0:T(1,128)S(1)} %select_n.108.in_slot_ref, s32[1,1024]{1,0:T(1,128)S(1)} %add.194.out_slot_ref, ...), custom_call_target="tpu_custom_call" | custom-call | tf_op jit(solution)/shard_map/pallas_call | solution.py:38
  76.5 1.0 copy-done.10
  77.5 0.7 copy-done.11
  78.2 0.7 copy-done.24
  78.9 0.7 copy-done.25
  79.6 0.7 copy-done.26
  80.3 9.4 %all-to-all-start.2 = ((bf16[128,8,512]{2,1,0:T(8,128)(2,1)}), bf16[128,8,512]{2,1,0:T(8,128)(2,1)S(1)}, u32[]{:S(2)}, u32[]{:S(2)}) async-start(bf16[128,8,512]{2,1,0:T(8,128)(2,1)} %copy-done.10), calls=%async_computation.2 | async-start | bytes 2097152 | tf_op jit(solution)/shard_map/all_to_all | solution.py:29
  89.7 1.9 %collective-permute-start.6 = (bf16[1024,128]{1,0:T(8,128)(2,1)}, bf16[1024,128]{1,0:T(8,128)(2,1)S(1)}, u32[]{:S(2)}, u32[]{:S(2)}) collective-permute-start(bf16[1024,128]{1,0:T(8,128)(2,1)} %copy-done.26), channel_id=1, source_target_pairs={{0,12},{4,0},{8,4},{12,8},{1,13},{5,1},{9,5},{13,9},{2,14},{6,2},{... | collective-permute-start | bytes 786440 | tf_op jit(solution)/shard_map/ppermute | solution.py:229
  91.6 0.6 collective-permute-start.7
  92.2 0.6 collective-permute-start.8
  92.7 1.0 copy-done.7
  93.7 1.0 copy-done.9
  94.7 0.7 copy-done.17
  95.4 0.7 copy-done.18
  96.1 0.7 copy-done.19
  96.8 4.7 %shard_map.132 = (bf16[32,256]{1,0:T(8,128)(2,1)}, bf16[32,256]{1,0:T(8,128)(2,1)}, f32[32,1792]{1,0:T(8,128)S(1)}) custom-call(s32[1]{0:T(128)} %bitcast.p_ref, s32[1]{0:T(128)} %copy.38.live_ref, bf16[256,1792]{1,0:T(8,128)(2,1)S(1)} %bitcast.28, bf16[256,1792]{1,0:T(8,128)(2,1)S(1)} %bitcast.25, f32[14,1,256]{2,1,0:T(1,128)S(1)} %bitcast.31, ...), custom_call_target="tpu_custom_call" | custom-call | tf_op jit(solution)/shard_map/pallas_call | solution.py:38
  101.5 1.8 %collective-permute-done.6.b_ref = bf16[1024,128]{1,0:T(8,128)(2,1)S(1)} collective-permute-done((bf16[1024,128]{1,0:T(8,128)(2,1)}, bf16[1024,128]{1,0:T(8,128)(2,1)S(1)}, u32[]{:S(2)}, u32[]{:S(2)}) %collective-permute-start.6) | collective-permute-done | bytes 262176 | tf_op jit(solution)/shard_map/ppermute | solution.py:229
  103.8 11.8 %collective-permute-done.8.d_ref = bf16[1024,128]{1,0:T(8,128)(2,1)S(1)} collective-permute-done((bf16[1024,128]{1,0:T(8,128)(2,1)}, bf16[1024,128]{1,0:T(8,128)(2,1)S(1)}, u32[]{:S(2)}, u32[]{:S(2)}) %collective-permute-start.8) | collective-permute-done | bytes 262176 | tf_op jit(solution)/shard_map/ppermute | solution.py:229
  115.8 1.2 collective-permute-start.9
  117.0 2.9 %collective-permute-start.10 = (bf16[256,128]{1,0:T(8,128)(2,1)S(1)}, bf16[256,128]{1,0:T(8,128)(2,1)S(1)}, u32[]{:S(2)}, u32[]{:S(2)}) collective-permute-start(bf16[256,128]{1,0:T(8,128)(2,1)S(1)} %get-tuple-element.49), channel_id=1, source_target_pairs={{0,16},{2,18},{16,0},{18,2},{1,17},{3,19},{17,1},{19,3},{4,20},{6,... | collective-permute-start | bytes 196616 | tf_op jit(solution)/shard_map/ppermute | solution.py:233
  120.0 2.8 %collective-permute-done.10.c_ref = bf16[256,128]{1,0:T(8,128)(2,1)S(1)} collective-permute-done((bf16[256,128]{1,0:T(8,128)(2,1)S(1)}, bf16[256,128]{1,0:T(8,128)(2,1)S(1)}, u32[]{:S(2)}, u32[]{:S(2)}) %collective-permute-start.10) | collective-permute-done | bytes 65568 | tf_op jit(solution)/shard_map/ppermute | solution.py:233
  122.8 1.7 %collective-permute-done.11.d_ref = bf16[256,128]{1,0:T(8,128)(2,1)S(1)} collective-permute-done((bf16[256,128]{1,0:T(8,128)(2,1)S(1)}, bf16[256,128]{1,0:T(8,128)(2,1)S(1)}, u32[]{:S(2)}, u32[]{:S(2)}) %collective-permute-start.11) | collective-permute-done | bytes 65568 | tf_op jit(solution)/shard_map/ppermute | solution.py:233
  124.4 0.7 shard_map.135
  125.1 0.9 copy-done.14
  126.0 0.8 shard_map.133
  (82 shorter events, 4.2 us)
Async XLA Ops:
  0.6 0.8 copy-start.20
  1.5 0.8 copy-start.21
  2.3 0.7 copy-start.22
  3.0 0.7 copy-start.23
  3.8 27.3 %collective-permute-start.2 = (bf16[256,128]{1,0:T(8,128)(2,1)S(1)}, bf16[256,128]{1,0:T(8,128)(2,1)S(1)}, u32[]{:S(2)}, u32[]{:S(2)}) collective-permute-start(bf16[256,128]{1,0:T(8,128)(2,1)S(1)} %get-tuple-element.32), channel_id=1, source_target_pairs={{0,18},{2,16},{16,2},{18,0},{1,19},{3,17},{17,3},{19,1},{4,22},{6,... | collective-permute-start | bytes 196616 | tf_op jit(solution)/shard_map/ppermute | solution.py:233
  7.4 23.7 %collective-permute-start.1 = (bf16[256,128]{1,0:T(8,128)(2,1)S(1)}, bf16[256,128]{1,0:T(8,128)(2,1)S(1)}, u32[]{:S(2)}, u32[]{:S(2)}) collective-permute-start(bf16[256,128]{1,0:T(8,128)(2,1)S(1)} %get-tuple-element.32), channel_id=1, source_target_pairs={{0,16},{2,18},{16,0},{18,2},{1,17},{3,19},{17,1},{19,3},{4,20},{6,... | collective-permute-start | bytes 196616 | tf_op jit(solution)/shard_map/ppermute | solution.py:233
  7.8 23.3 %collective-permute-start = (bf16[384,128]{1,0:T(8,128)(2,1)S(1)}, bf16[384,128]{1,0:T(8,128)(2,1)S(1)}, u32[]{:S(2)}, u32[]{:S(2)}) collective-permute-start(bf16[384,128]{1,0:T(8,128)(2,1)S(1)} %get-tuple-element.31), channel_id=1, source_target_pairs={{0,2},{2,0},{16,18},{18,16},{1,3},{3,1},{17,19},{19,17},{4,6},{6,4... | collective-permute-start | bytes 294920 | tf_op jit(solution)/shard_map/ppermute | solution.py:233
  8.8 1.2 copy-start
  9.9 1.2 copy-start.2
  11.1 1.2 copy-start.4
  12.3 0.7 copy-start.15
  13.0 12.3 %copy-start.3 = (bf16[1,256,1792]{2,1,0:T(8,128)(2,1)S(1)}, bf16[1,256,1792]{2,1,0:T(8,128)(2,1)}, u32[]{:S(2)}) copy-start(bf16[1,256,1792]{2,1,0:T(8,128)(2,1)} %param.10) | copy-start | bytes 2752516
  14.5 22.0 %all-to-all-start = ((bf16[16,8,1024]{2,1,0:T(8,128)(2,1)}), bf16[16,8,1024]{2,1,0:T(8,128)(2,1)S(1)}, u32[]{:S(2)}, u32[]{:S(2)}) async-start(bf16[16,8,1024]{2,1,0:T(8,128)(2,1)} %bitcast.6), calls=%async_computation | async-start | bytes 524288 | tf_op jit(solution)/shard_map/all_to_all | solution.py:29
  25.3 1.4 %copy-start.1 = (bf16[1,256,1792]{2,1,0:T(8,128)(2,1)S(1)}, bf16[1,256,1792]{2,1,0:T(8,128)(2,1)}, u32[]{:S(2)}) copy-start(bf16[1,256,1792]{2,1,0:T(8,128)(2,1)} %param.11) | copy-start | bytes 2752516
  26.7 1.3 %copy-start.16 = (f32[1,14,256]{2,0,1:T(1,128)S(1)}, f32[1,14,256]{2,0,1:T(1,128)}, u32[]{:S(2)}) copy-start(f32[1,14,256]{2,0,1:T(1,128)} %param.12) | copy-start | bytes 43012
  26.7 2.1 %copy-start.27 = (bf16[1,256,1792]{1,2,0:T(8,128)(2,1)S(1)}, bf16[1,256,1792]{1,2,0:T(8,128)(2,1)}, u32[]{:S(2)}) copy-start(bf16[1,256,1792]{1,2,0:T(8,128)(2,1)} %copy.29) | copy-start | bytes 2752516
  31.1 13.3 %copy-start.28 = (s32[2]{0:T(128)}, s32[2]{0:T(128)S(1)}, u32[]{:S(2)}) copy-start(s32[2]{0:T(128)S(1)} %iota_multiply_fusion) | copy-start | bytes 28
  31.2 33.0 %collective-permute-start.5 = (bf16[1280,128]{1,0:T(8,128)(2,1)S(1)}, bf16[1280,128]{1,0:T(8,128)(2,1)S(1)}, u32[]{:S(2)}, u32[]{:S(2)}) collective-permute-start(bf16[1280,128]{1,0:T(8,128)(2,1)S(1)} %slice_dynamic-update-slice_fusion.2.refs_0_.kv0_ref), channel_id=1, source_target_pairs={{0,12},{4,0},{8,4},{12,8},{1,13},{5,1},{9,5},{13,9},{2,14},{6,2},{... | collective-permute-start | bytes 983048 | tf_op jit(solution)/shard_map/ppermute | solution.py:229
  33.7 30.4 %collective-permute-start.4 = (bf16[1280,128]{1,0:T(8,128)(2,1)S(1)}, bf16[1280,128]{1,0:T(8,128)(2,1)S(1)}, u32[]{:S(2)}, u32[]{:S(2)}) collective-permute-start(bf16[1280,128]{1,0:T(8,128)(2,1)S(1)} %slice_dynamic-update-slice_fusion.2.refs_0_.kv0_ref), channel_id=1, source_target_pairs={{0,8},{4,12},{8,0},{12,4},{1,9},{5,13},{9,1},{13,5},{2,10},{6,14},... | collective-permute-start | bytes 983048 | tf_op jit(solution)/shard_map/ppermute | solution.py:229
  34.3 29.9 %collective-permute-start.3 = (bf16[1280,128]{1,0:T(8,128)(2,1)S(1)}, bf16[1280,128]{1,0:T(8,128)(2,1)S(1)}, u32[]{:S(2)}, u32[]{:S(2)}) collective-permute-start(bf16[1280,128]{1,0:T(8,128)(2,1)S(1)} %slice_dynamic-update-slice_fusion.2.refs_0_.kv0_ref), channel_id=1, source_target_pairs={{0,4},{4,8},{8,12},{12,0},{1,5},{5,9},{9,13},{13,1},{2,6},{6,10},{... | collective-permute-start | bytes 983048 | tf_op jit(solution)/shard_map/ppermute | solution.py:229
  38.7 25.5 %all-to-all-start.1 = ((bf16[8,48,1024]{2,1,0:T(8,128)(2,1)}), bf16[8,48,1024]{2,1,0:T(8,128)(2,1)S(1)}, u32[]{:S(2)}, u32[]{:S(2)}) async-start(bf16[8,48,1024]{2,1,0:T(8,128)(2,1)} %shard_map.129), calls=%async_computation.1 | async-start | bytes 1572864 | tf_op jit(solution)/shard_map/all_to_all | solution.py:29
  64.2 12.3 %copy-start.6 = (bf16[1280,128]{1,0:T(8,128)(2,1)}, bf16[1280,128]{1,0:T(8,128)(2,1)S(1)}, u32[]{:S(2)}) copy-start(bf16[1280,128]{1,0:T(8,128)(2,1)S(1)} %collective-permute-done.4.refs_2_.kv2_ref) | copy-start | bytes 983044
  64.2 12.3 %copy-start.8 = (bf16[1280,128]{1,0:T(8,128)(2,1)}, bf16[1280,128]{1,0:T(8,128)(2,1)S(1)}, u32[]{:S(2)}) copy-start(bf16[1280,128]{1,0:T(8,128)(2,1)S(1)} %collective-permute-done.3.refs_1_.kv1_ref) | copy-start | bytes 983044
  76.5 1.0 copy-start.10
  77.5 0.7 copy-start.11
  78.2 0.7 copy-start.24
  78.9 0.7 copy-start.25
  79.6 0.7 copy-start.26
  80.3 12.4 %copy-start.5 = (bf16[1,256,1792]{2,1,0:T(8,128)(2,1)S(1)}, bf16[1,256,1792]{2,1,0:T(8,128)(2,1)}, u32[]{:S(2)}) copy-start(bf16[1,256,1792]{2,1,0:T(8,128)(2,1)} %param.9) | copy-start | bytes 2752516
  80.3 44.7 %all-to-all-start.2 = ((bf16[128,8,512]{2,1,0:T(8,128)(2,1)}), bf16[128,8,512]{2,1,0:T(8,128)(2,1)S(1)}, u32[]{:S(2)}, u32[]{:S(2)}) async-start(bf16[128,8,512]{2,1,0:T(8,128)(2,1)} %copy-done.10), calls=%async_computation.2 | async-start | bytes 2097152 | tf_op jit(solution)/shard_map/all_to_all | solution.py:29
  89.7 13.5 %collective-permute-start.6 = (bf16[1024,128]{1,0:T(8,128)(2,1)}, bf16[1024,128]{1,0:T(8,128)(2,1)S(1)}, u32[]{:S(2)}, u32[]{:S(2)}) collective-permute-start(bf16[1024,128]{1,0:T(8,128)(2,1)} %copy-done.26), channel_id=1, source_target_pairs={{0,12},{4,0},{8,4},{12,8},{1,13},{5,1},{9,5},{13,9},{2,14},{6,2},{... | collective-permute-start | bytes 786440 | tf_op jit(solution)/shard_map/ppermute | solution.py:229
  91.6 12.2 %collective-permute-start.7 = (bf16[1024,128]{1,0:T(8,128)(2,1)}, bf16[1024,128]{1,0:T(8,128)(2,1)S(1)}, u32[]{:S(2)}, u32[]{:S(2)}) collective-permute-start(bf16[1024,128]{1,0:T(8,128)(2,1)} %copy-done.25), channel_id=1, source_target_pairs={{0,8},{4,12},{8,0},{12,4},{1,9},{5,13},{9,1},{13,5},{2,10},{6,14},... | collective-permute-start | bytes 786440 | tf_op jit(solution)/shard_map/ppermute | solution.py:229
  92.2 23.5 %collective-permute-start.8 = (bf16[1024,128]{1,0:T(8,128)(2,1)}, bf16[1024,128]{1,0:T(8,128)(2,1)S(1)}, u32[]{:S(2)}, u32[]{:S(2)}) collective-permute-start(bf16[1024,128]{1,0:T(8,128)(2,1)} %copy-done.24), channel_id=1, source_target_pairs={{0,4},{4,8},{8,12},{12,0},{1,5},{5,9},{9,13},{13,1},{2,6},{6,10},{... | collective-permute-start | bytes 786440 | tf_op jit(solution)/shard_map/ppermute | solution.py:229
  92.7 1.0 copy-start.7
  93.7 1.0 copy-start.9
  94.7 0.7 copy-start.17
  95.4 0.7 copy-start.18
  96.1 0.7 copy-start.19
  96.8 18.8 %copy-start.12 = (bf16[1024,128]{1,0:T(8,128)(2,1)S(1)}, bf16[1024,128]{1,0:T(8,128)(2,1)}, u32[]{:S(2)}) copy-start(bf16[1024,128]{1,0:T(8,128)(2,1)} %copy-done.11) | copy-start | bytes 786436
  101.5 22.9 %copy-start.13 = (f32[32,1792]{1,0:T(8,128)}, f32[32,1792]{1,0:T(8,128)S(1)}, u32[]{:S(2)}) copy-start(f32[32,1792]{1,0:T(8,128)S(1)} %get-tuple-element.42.own_ref) | copy-start | bytes 688132
  115.8 4.2 %collective-permute-start.9 = (bf16[256,128]{1,0:T(8,128)(2,1)S(1)}, bf16[256,128]{1,0:T(8,128)(2,1)S(1)}, u32[]{:S(2)}, u32[]{:S(2)}) collective-permute-start(bf16[256,128]{1,0:T(8,128)(2,1)S(1)} %get-tuple-element.48), channel_id=1, source_target_pairs={{0,2},{2,0},{16,18},{18,16},{1,3},{3,1},{17,19},{19,17},{4,6},{6,4... | collective-permute-start | bytes 196616 | tf_op jit(solution)/shard_map/ppermute | solution.py:233
  117.0 5.7 %collective-permute-start.10 = (bf16[256,128]{1,0:T(8,128)(2,1)S(1)}, bf16[256,128]{1,0:T(8,128)(2,1)S(1)}, u32[]{:S(2)}, u32[]{:S(2)}) collective-permute-start(bf16[256,128]{1,0:T(8,128)(2,1)S(1)} %get-tuple-element.49), channel_id=1, source_target_pairs={{0,16},{2,18},{16,0},{18,2},{1,17},{3,19},{17,1},{19,3},{4,20},{6,... | collective-permute-start | bytes 196616 | tf_op jit(solution)/shard_map/ppermute | solution.py:233
  120.0 4.5 %collective-permute-start.11 = (bf16[256,128]{1,0:T(8,128)(2,1)S(1)}, bf16[256,128]{1,0:T(8,128)(2,1)S(1)}, u32[]{:S(2)}, u32[]{:S(2)}) collective-permute-start(bf16[256,128]{1,0:T(8,128)(2,1)S(1)} %get-tuple-element.50), channel_id=1, source_target_pairs={{0,18},{2,16},{16,2},{18,0},{1,19},{3,17},{17,3},{19,1},{4,22},{6,... | collective-permute-start | bytes 196616 | tf_op jit(solution)/shard_map/ppermute | solution.py:233
  125.1 0.9 copy-start.14
where the time goes:
time: 128 us; the launch traced here: 127 us
  starting transfers between devices  40.2 us (31%)
  waiting for transfers between devices  38.8 us (30%)
  Pallas kernels  21.5 us (17%)
  local copies, waits for them, and re-layouts  21 us (16%)
  other arithmetic  3.78 us (3%)
  between operations  1.56 us (1%)
    all_to_all x3, starting transfers between devices, exchange(): return lax.all_to_all(tiles, axes, split_axis=0, concat_axis=0, tiled=True)  25 us
    pallas_call x8, Pallas kernels, call(): pl.pallas_call(body, out_shape=out_shape, interpret=INTERPRET, compiler_p...  21.5 us
    all_to_all x3, waiting for transfers between devices, exchange(): return lax.all_to_all(tiles, axes, split_axis=0, concat_axis=0, tiled=True)  20.2 us
    unnamed x65, local copies, waits for them, and re-layouts  18.9 us
    ppermute x6, waiting for transfers between devices, shifted(): return lax.ppermute(value, ALONG_X, [(k, (k + by) % 4) for k in range(4)])  14.2 us
    ppermute x6, starting transfers between devices, crossed(): return lax.ppermute(value, ALONG_Y, [(k, k ^ by) for k in range(4)])  8.47 us
    ppermute x6, starting transfers between devices, shifted(): return lax.ppermute(value, ALONG_X, [(k, (k + by) % 4) for k in range(4)])  6.7 us
    ppermute x6, waiting for transfers between devices, crossed(): return lax.ppermute(value, ALONG_Y, [(k, k ^ by) for k in range(4)])  4.46 us
  transfers between devices with their start and end apart: 15, of which 7 were waited for; matrix products, arithmetic and copies ran while one was open for 7% of the time, Pallas kernels for 7%

commit v1 on v0

--- a/solution.py
+++ b/solution.py
@@ -23,6 +23,7 @@
 BF16 = jnp.bfloat16
 F32 = jnp.float32
 SCALE = 1.0 / math.sqrt(HEAD_WIDTH)
+EXACT = lax.Precision.HIGHEST
 
 
 def exchange(tiles, axes):
@@ -33,8 +34,8 @@
     return lax.dot_general(a, b, (((ca,), (cb,)), ((), ())), preferred_element_type=F32)
 
 
-def call(body, out_shape, *args, **kw):
-    params = pltpu.CompilerParams(vmem_limit_bytes=VMEM_BYTES)
+def call(body, out_shape, *args, small=True, **kw):
+    params = pltpu.CompilerParams(vmem_limit_bytes=VMEM_BYTES if small else None)
     return pl.pallas_call(
         body, out_shape=out_shape, interpret=INTERPRET, compiler_params=params, **kw
     )(*args)
@@ -169,6 +170,7 @@
         out_slot,
         rows,
         *kv,
+        small=False,
         scratch_shapes=[
             pltpu.VMEM((1024, 2 * HEAD_WIDTH), BF16),
             pltpu.VMEM((1024, 2 * HEAD_WIDTH), BF16),
@@ -234,8 +236,8 @@
 
 
 def self_kernel(
-    p_ref, live_ref, q_ref, g_ref, norm_ref, delta_ref, col_norm_ref, col_delta_ref, kv0_ref, kv1_ref, kv2_ref,
-    kv3_ref, gk_ref, gv_ref, gq_ref,
+    p_ref, live_ref, q_ref, o_ref, g_ref, norm_ref, kv0_ref, kv1_ref, kv2_ref, kv3_ref,
+    gk_ref, gv_ref, gq_ref,
 ):
     p, live = p_ref[0], live_ref[0]
     rows_total = q_ref.shape[0]
@@ -244,6 +246,9 @@
     live_row = lax.broadcasted_iota(jnp.int32, (rows_total, HEAD_WIDTH), 0) < live
     live_own = lax.broadcasted_iota(jnp.int32, (32, HEAD_WIDTH), 0) + p * 32 < live
     zero = jnp.zeros((), BF16)
+    ones = jnp.ones((8, HEAD_WIDTH), F32)
+    own = pl.ds(pl.multiple_of(p * 32, 32), 32)
+    diagonal = i_row == j_row
     kv_refs = (kv0_ref, kv1_ref, kv2_ref, kv3_ref)
     lane = lax.broadcasted_iota(jnp.int32, (1, rows_total), 1)
     block = lane // 32
@@ -266,18 +271,24 @@
             lanes = slice(head * HEAD_WIDTH, (head + 1) * HEAD_WIDTH)
             q = q_ref[:, lanes]
             g = jnp.where(live_row, g_ref[:, lanes], zero)
+            product = g.astype(F32) * o_ref[:, lanes].astype(F32)
+            delta = lax.dot_general(
+                ones, product, (((1,), (1,)), ((), ())), precision=EXACT, preferred_element_type=F32
+            )
             prob = jnp.exp(dot(keys, q, 1, 1) * SCALE - norm_ref[head])
             prob = jnp.where(j_row <= i_row, prob, 0.0)
-            sgrad = prob * (dot(values, g, 1, 1) - delta_ref[head : head + 1, :])
+            sgrad = prob * (dot(values, g, 1, 1) - delta[0:1, :])
             gv = gv + dot(prob.astype(BF16), g, 1, 0)
             gk = gk + dot(sgrad.astype(BF16), q, 1, 0)
-            q_own = q_ref[pl.ds(pl.multiple_of(p * 32, 32), 32), lanes]
-            g_own = g_ref[pl.ds(pl.multiple_of(p * 32, 32), 32), lanes]
+            q_own, g_own = q_ref[own, lanes], g_ref[own, lanes]
             g_own = jnp.where(live_own, g_own, zero)
-            prob = jnp.exp(dot(q_own, all_keys, 1, 1) * SCALE - col_norm_ref[:, head : head + 1])
+            product = g_own.astype(F32) * o_ref[own, lanes].astype(F32)
+            delta_own = jnp.sum(product, axis=1, keepdims=True)
+            norm_own = jnp.sum(jnp.where(diagonal, norm_ref[head], 0.0), axis=1, keepdims=True)
+            prob = jnp.exp(dot(q_own, all_keys, 1, 1) * SCALE - norm_own)
             i_own = lax.broadcasted_iota(jnp.int32, prob.shape, 0) + p * 32
             prob = jnp.where(position <= i_own, prob, 0.0)
-            sgrad = prob * (dot(g_own, all_values, 1, 1) - col_delta_ref[:, head : head + 1])
+            sgrad = prob * (dot(g_own, all_values, 1, 1) - delta_own)
             gq_ref[:, lanes] = dot(sgrad.astype(BF16), all_keys, 1, 0) * SCALE
         gk_ref[:, key_lanes] = (gk * SCALE).astype(BF16)
         gv_ref[:, key_lanes] = gv.astype(BF16)
@@ -304,7 +315,6 @@
     class_rows = slice_rows // CLASSES
     q, o, g = queries[0], outputs[0], grad_out[0]
     norms = log_norms.transpose(1, 0, 2)
-    live = lengths[0]
     smem, vmem = pl.BlockSpec(memory_space=pltpu.SMEM), pl.BlockSpec(memory_space=pltpu.VMEM)
 
     picked = call(
@@ -318,6 +328,7 @@
         g,
         norms,
         in_specs=[smem] * 3 + [vmem] * 4,
+        small=False,
     )
     arrived = exchange(picked.reshape(16, 8, 1024), SAMPLE)
 
@@ -368,17 +379,7 @@
     out_slot = slot_of.reshape(16, spans, 1, 4) + LIVE * jnp.arange(2)[None, None, :, None]
     out_slot = out_slot.reshape(1, 1024)
 
-    live_rows = lax.broadcasted_iota(jnp.int32, (slice_rows, 1), 0) < live
-    g_live = jnp.where(live_rows, g, jnp.zeros((), BF16))
-    delta = jnp.sum(
-        (g_live.astype(F32) * o.astype(F32)).reshape(slice_rows, heads, HEAD_WIDTH), axis=-1
-    ).T
     own_rows = slice_rows // spans
-    col_norms = lax.dynamic_slice_in_dim(log_norms[0], p * own_rows, own_rows, 1).T
-    col_delta = lax.dynamic_slice_in_dim(delta, p * own_rows, own_rows, 1).T
-    rows, delta, col_norms, col_delta = lax.optimization_barrier(
-        (rows, delta, col_norms, col_delta)
-    )
     own_shape = jax.ShapeDtypeStruct((own_rows, 2 * HEAD_WIDTH), BF16)
     gk_self, gv_self, gq_self = call(
         self_kernel,
@@ -386,18 +387,17 @@
         p[None],
         lengths,
         q,
+        o,
         g,
         norms,
-        delta,
-        col_norms,
-        col_delta,
         *kv,
-        in_specs=[smem] * 2 + [vmem] * 10,
+        in_specs=[smem] * 2 + [vmem] * 8,
+        small=False,
     )
 
     kv_grads, gq_parts = prompt_terms(in_slot, out_slot, rows, *kv)
+    parts = [kv_grads[0]] + [shifted(kv_grads[k], -k) for k in (1, 2, 3)]
     gq_parts = exchange(gq_parts, SAMPLE_SPAN)
-    parts = [kv_grads[0]] + [shifted(kv_grads[k], -k) for k in (1, 2, 3)]
     *parts, gq_self = lax.optimization_barrier((*parts, gq_self))
     parts = call(x_sum_kernel, [packed(256)] * 4, *parts)
     parts = [parts[0]] + [crossed(parts[k], k) for k in (1, 2, 3)]

time: 128 us -> 121 us (0.945)
  local copies, waits for them, and re-layouts: 21 us -> 5.76 us
  Pallas kernels: 21.5 us -> 30.6 us
  waiting for transfers between devices: 38.8 us -> 43.2 us
  starting transfers between devices: 40.2 us -> 37.6 us
  other arithmetic: 3.78 us -> 1.6 us
    unnamed x65 -> x33, local copies, waits for them, and re-layouts: 18.9 us -> 4.09 us
    pallas_call x8, Pallas kernels: 21.5 us -> 30.6 us  [call(): pl.pallas_call(body, out_shape=out_shape, interpret=INTERPRET, compiler_p...]
    all_to_all x3, waiting for transfers between devices: 20.2 us -> 23.8 us  [exchange(): return lax.all_to_all(tiles, axes, split_axis=0, concat_axis=0, tiled=True)]
    all_to_all x3, starting transfers between devices: 25 us -> 22.4 us  [exchange(): return lax.all_to_all(tiles, axes, split_axis=0, concat_axis=0, tiled=True)]
    reduce_sum x1 -> x0, other arithmetic: 1.5 us -> none  [shards(): jnp.sum((g_live.astype(F32) * o.astype(F32)).reshape(slice_rows, heads, H...]
  transfers between devices with their start and end apart: 15 -> 15, of which waited for: 7 -> 8; matrix products, arithmetic and copies ran while one was open for 7% -> 3% of each run, Pallas kernels for 7% -> 12%
where the time goes in v1:
time: 121 us; the launch traced here: 120 us
  waiting for transfers between devices  43.2 us (36%)
  starting transfers between devices  37.6 us (31%)
  Pallas kernels  30.6 us (25%)
  local copies, waits for them, and re-layouts  5.76 us (5%)
  other arithmetic  1.6 us (1%)
  between operations  1.53 us (1%)
    pallas_call x8, Pallas kernels, call(): pl.pallas_call(body, out_shape=out_shape, interpret=INTERPRET, compiler_p...  30.6 us
    all_to_all x3, waiting for transfers between devices, exchange(): return lax.all_to_all(tiles, axes, split_axis=0, concat_axis=0, tiled=True)  23.8 us
    all_to_all x3, starting transfers between devices, exchange(): return lax.all_to_all(tiles, axes, split_axis=0, concat_axis=0, tiled=True)  22.4 us
    ppermute x6, waiting for transfers between devices, shifted(): return lax.ppermute(value, ALONG_X, [(k, (k + by) % 4) for k in range(4)])  14.9 us
    ppermute x6, starting transfers between devices, crossed(): return lax.ppermute(value, ALONG_Y, [(k, k ^ by) for k in range(4)])  8.49 us
    ppermute x6, starting transfers between devices, shifted(): return lax.ppermute(value, ALONG_X, [(k, (k + by) % 4) for k in range(4)])  6.7 us
    ppermute x6, waiting for transfers between devices, crossed(): return lax.ppermute(value, ALONG_Y, [(k, k ^ by) for k in range(4)])  4.46 us
    unnamed x33, local copies, waits for them, and re-layouts  4.09 us
  transfers between devices with their start and end apart: 15, of which 8 were waited for; matrix products, arithmetic and copies ran while one was open for 3% of the time, Pallas kernels for 12%

profile of v1, /device:TPU:1, one launch (start us, length us, event | category | flops | bytes accessed | tf_op | source)
XLA Modules:
  0.0 120.2 jit_solution(10719367697461390049)
XLA Ops:
  0.6 0.8 copy-done.2
  1.5 0.8 copy-done.3
  2.3 0.7 copy-done.4
  3.0 0.7 copy-done.5
  3.8 3.6 %collective-permute-start.2 = (bf16[256,128]{1,0:T(8,128)(2,1)S(1)}, bf16[256,128]{1,0:T(8,128)(2,1)S(1)}, u32[]{:S(2)}, u32[]{:S(2)}) collective-permute-start(bf16[256,128]{1,0:T(8,128)(2,1)S(1)} %get-tuple-element.27), channel_id=1, source_target_pairs={{0,18},{2,16},{16,2},{18,0},{1,19},{3,17},{17,3},{19,1},{4,22},{6,... | collective-permute-start | bytes 196616 | tf_op jit(solution)/shard_map/ppermute | solution.py:235
  7.4 0.3 collective-permute-start.1
  7.8 0.3 collective-permute-start
  8.8 3.2 %shard_map.128 = bf16[8,2,8,1024]{3,2,1,0:T(8,128)(2,1)} custom-call(s32[1]{0:T(128)} %bitcast.p_ref, s32[1]{0:T(128)} %bitcast.1.turn_ref, s32[1]{0:T(128)S(6)} %copy.22.live_ref, bf16[256,1792]{1,0:T(8,128)(2,1)} %bitcast.17, bf16[256,1792]{1,0:T(8,128)(2,1)} %bitcast.19, bf16[256,1792]{1,0:T(8,128)(2,1)} %bitcast.21, f32[14,1,256]{2,1,0:T(1,128)} %bitcast.26), custom_call_target="tpu_custom_call" | custom-call | tf_op jit(solution)/shard_map/pallas_call | solution.py:39
  12.0 10.8 %all-to-all-start = ((bf16[16,8,1024]{2,1,0:T(8,128)(2,1)}), bf16[16,8,1024]{2,1,0:T(8,128)(2,1)S(1)}, u32[]{:S(2)}, u32[]{:S(2)}) async-start(bf16[16,8,1024]{2,1,0:T(8,128)(2,1)} %bitcast.23), calls=%async_computation | async-start | bytes 524288 | tf_op jit(solution)/shard_map/all_to_all | solution.py:30
  23.0 2.6 %collective-permute-start.5 = (bf16[1280,128]{1,0:T(8,128)(2,1)S(1)}, bf16[1280,128]{1,0:T(8,128)(2,1)S(1)}, u32[]{:S(2)}, u32[]{:S(2)}) collective-permute-start(bf16[1280,128]{1,0:T(8,128)(2,1)S(1)} %slice_dynamic-update-slice_fusion.2.refs_0_.kv0_ref), channel_id=1, source_target_pairs={{0,12},{4,0},{8,4},{12,8},{1,13},{5,1},{9,5},{13,9},{2,14},{6,2},{... | collective-permute-start | bytes 983048 | tf_op jit(solution)/shard_map/ppermute | solution.py:231
  25.5 0.5 collective-permute-start.4
  26.0 0.6 collective-permute-start.3
  26.6 7.4 %all-to-all-done.rows_ref = bf16[16,8,1024]{2,1,0:T(8,128)(2,1)S(1)} async-done(((bf16[16,8,1024]{2,1,0:T(8,128)(2,1)}), bf16[16,8,1024]{2,1,0:T(8,128)(2,1)S(1)}, u32[]{:S(2)}, u32[]{:S(2)}) %all-to-all-start) | async-done | bytes 262176 | tf_op jit(solution)/shard_map/all_to_all | solution.py:30
  34.0 0.5 fusion.5
  34.5 0.1 fusion.11
  34.6 0.1 select_reduce_fusion.2
  34.7 1.4 %shard_map.129 = bf16[8,48,1024]{2,1,0:T(8,128)(2,1)} custom-call(s32[1]{0:T(128)} %bitcast.p_ref, s32[1]{0:T(128)} %bitcast.8.z_ref, bf16[16,8,1024]{2,1,0:T(8,128)(2,1)S(1)} %all-to-all-done.rows_ref), custom_call_target="tpu_custom_call" | custom-call | tf_op jit(solution)/shard_map/pallas_call | solution.py:39
  36.2 3.5 %all-to-all-start.1 = ((bf16[8,48,1024]{2,1,0:T(8,128)(2,1)}), bf16[8,48,1024]{2,1,0:T(8,128)(2,1)S(1)}, u32[]{:S(2)}, u32[]{:S(2)}) async-start(bf16[8,48,1024]{2,1,0:T(8,128)(2,1)} %shard_map.129), calls=%async_computation.1 | async-start | bytes 1572864 | tf_op jit(solution)/shard_map/all_to_all | solution.py:30
  39.7 0.3 select_reduce_fusion.1
  40.1 0.1 select_reduce_fusion
  40.2 0.1 copy.15
  40.3 0.1 iota_compare_fusion.3
  40.3 0.1 iota_add_fusion
  40.4 0.1 add_select_fusion
  40.5 0.1 add_select_fusion.2
  40.6 0.7 select_n.95.in_slot_ref
  41.2 0.1 copy.16
  41.4 0.1 broadcast_add_fusion
  41.5 0.8 add.190.out_slot_ref
  42.3 1.4 %collective-permute-done.3.refs_1_.kv1_ref = bf16[1280,128]{1,0:T(8,128)(2,1)S(1)} collective-permute-done((bf16[1280,128]{1,0:T(8,128)(2,1)S(1)}, bf16[1280,128]{1,0:T(8,128)(2,1)S(1)}, u32[]{:S(2)}, u32[]{:S(2)}) %collective-permute-start.3) | collective-permute-done | bytes 327712 | tf_op jit(solution)/shard_map/ppermute | solution.py:231
  43.7 16.5 %all-to-all-done.1.rows_ref = bf16[8,48,1024]{2,1,0:T(8,128)(2,1)S(1)} async-done(((bf16[8,48,1024]{2,1,0:T(8,128)(2,1)}), bf16[8,48,1024]{2,1,0:T(8,128)(2,1)S(1)}, u32[]{:S(2)}, u32[]{:S(2)}) %all-to-all-start.1) | async-done | bytes 786464 | tf_op jit(solution)/shard_map/all_to_all | solution.py:30
  60.2 0.9 copy-done.6
  61.0 14.9 %shard_map.131 = (bf16[1024,128]{1,0:T(8,128)(2,1)}, bf16[1024,128]{1,0:T(8,128)(2,1)}, bf16[1024,128]{1,0:T(8,128)(2,1)}, bf16[1024,128]{1,0:T(8,128)(2,1)}, bf16[128,8,512]{2,1,0:T(8,128)(2,1)}) custom-call(s32[1,384]{1,0:T(1,128)} %select_n.95.in_slot_ref, s32[1,1024]{1,0:T(1,128)} %add.190.out_slot_ref, bf16[8,48,1024]{2,1,0:T(8,128)(2,1)} %copy-done.6, ...), custom_call_target="tpu_custom_call" | custom-call | tf_op jit(solution)/shard_map/pallas_call | solution.py:39
  75.9 8.1 %all-to-all-start.2 = ((bf16[128,8,512]{2,1,0:T(8,128)(2,1)}), bf16[128,8,512]{2,1,0:T(8,128)(2,1)S(1)}, u32[]{:S(2)}, u32[]{:S(2)}) async-start(bf16[128,8,512]{2,1,0:T(8,128)(2,1)} %get-tuple-element.28), calls=%async_computation.2 | async-start | bytes 2097152 | tf_op jit(solution)/shard_map/all_to_all | solution.py:30
  84.1 1.9 %collective-permute-start.6 = (bf16[1024,128]{1,0:T(8,128)(2,1)S(1)}, bf16[1024,128]{1,0:T(8,128)(2,1)S(1)}, u32[]{:S(2)}, u32[]{:S(2)}) collective-permute-start(bf16[1024,128]{1,0:T(8,128)(2,1)S(1)} %copy-done.13), channel_id=1, source_target_pairs={{0,12},{4,0},{8,4},{12,8},{1,13},{5,1},{9,5},{13,9},{2,14},{6,2},{... | collective-permute-start | bytes 786440 | tf_op jit(solution)/shard_map/ppermute | solution.py:231
  85.9 0.6 collective-permute-start.7
  86.5 0.6 collective-permute-start.8
  87.1 9.4 %shard_map.132 = (bf16[32,256]{1,0:T(8,128)(2,1)}, bf16[32,256]{1,0:T(8,128)(2,1)}, f32[32,1792]{1,0:T(8,128)}) custom-call(s32[1]{0:T(128)} %bitcast.p_ref, s32[1]{0:T(128)S(6)} %copy.22.live_ref, bf16[256,1792]{1,0:T(8,128)(2,1)} %bitcast.18, bf16[256,1792]{1,0:T(8,128)(2,1)} %bitcast.20, bf16[256,1792]{1,0:T(8,128)(2,1)} %bitcast.22, ...), custom_call_target="tpu_custom_call" | custom-call | tf_op jit(solution)/shard_map/pallas_call | solution.py:39
  96.5 0.2 collective-permute-done.6.b_ref
  96.7 1.7 %collective-permute-done.7.c_ref = bf16[1024,128]{1,0:T(8,128)(2,1)S(1)} collective-permute-done((bf16[1024,128]{1,0:T(8,128)(2,1)S(1)}, bf16[1024,128]{1,0:T(8,128)(2,1)S(1)}, u32[]{:S(2)}, u32[]{:S(2)}) %collective-permute-start.7) | collective-permute-done | bytes 262176 | tf_op jit(solution)/shard_map/ppermute | solution.py:231
  98.4 11.6 %collective-permute-done.8.d_ref = bf16[1024,128]{1,0:T(8,128)(2,1)S(1)} collective-permute-done((bf16[1024,128]{1,0:T(8,128)(2,1)S(1)}, bf16[1024,128]{1,0:T(8,128)(2,1)S(1)}, u32[]{:S(2)}, u32[]{:S(2)}) %collective-permute-start.8) | collective-permute-done | bytes 262176 | tf_op jit(solution)/shard_map/ppermute | solution.py:231
  110.0 0.1 shard_map.134
  110.1 1.3 %collective-permute-start.9 = (bf16[256,128]{1,0:T(8,128)(2,1)S(1)}, bf16[256,128]{1,0:T(8,128)(2,1)S(1)}, u32[]{:S(2)}, u32[]{:S(2)}) collective-permute-start(bf16[256,128]{1,0:T(8,128)(2,1)S(1)} %get-tuple-element.40), channel_id=1, source_target_pairs={{0,2},{2,0},{16,18},{18,16},{1,3},{3,1},{17,19},{19,17},{4,6},{6,4... | collective-permute-start | bytes 196616 | tf_op jit(solution)/shard_map/ppermute | solution.py:235
  111.4 2.9 %collective-permute-start.10 = (bf16[256,128]{1,0:T(8,128)(2,1)S(1)}, bf16[256,128]{1,0:T(8,128)(2,1)S(1)}, u32[]{:S(2)}, u32[]{:S(2)}) collective-permute-start(bf16[256,128]{1,0:T(8,128)(2,1)S(1)} %get-tuple-element.41), channel_id=1, source_target_pairs={{0,16},{2,18},{16,0},{18,2},{1,17},{3,19},{17,1},{19,3},{4,20},{6,... | collective-permute-start | bytes 196616 | tf_op jit(solution)/shard_map/ppermute | solution.py:235
  114.3 2.8 %collective-permute-done.10.c_ref = bf16[256,128]{1,0:T(8,128)(2,1)S(1)} collective-permute-done((bf16[256,128]{1,0:T(8,128)(2,1)S(1)}, bf16[256,128]{1,0:T(8,128)(2,1)S(1)}, u32[]{:S(2)}, u32[]{:S(2)}) %collective-permute-start.10) | collective-permute-done | bytes 65568 | tf_op jit(solution)/shard_map/ppermute | solution.py:235
  117.1 1.7 %collective-permute-done.11.d_ref = bf16[256,128]{1,0:T(8,128)(2,1)S(1)} collective-permute-done((bf16[256,128]{1,0:T(8,128)(2,1)S(1)}, bf16[256,128]{1,0:T(8,128)(2,1)S(1)}, u32[]{:S(2)}, u32[]{:S(2)}) %collective-permute-start.11) | collective-permute-done | bytes 65568 | tf_op jit(solution)/shard_map/ppermute | solution.py:235
  118.7 0.7 shard_map.135
  119.4 0.8 shard_map.133
  (44 shorter events, 0.2 us)
Async XLA Ops:
  0.6 0.8 copy-start.2
  1.5 0.8 copy-start.3
  2.3 0.7 copy-start.4
  3.0 0.7 copy-start.5
  3.8 19.1 %collective-permute-start.2 = (bf16[256,128]{1,0:T(8,128)(2,1)S(1)}, bf16[256,128]{1,0:T(8,128)(2,1)S(1)}, u32[]{:S(2)}, u32[]{:S(2)}) collective-permute-start(bf16[256,128]{1,0:T(8,128)(2,1)S(1)} %get-tuple-element.27), channel_id=1, source_target_pairs={{0,18},{2,16},{16,2},{18,0},{1,19},{3,17},{17,3},{19,1},{4,22},{6,... | collective-permute-start | bytes 196616 | tf_op jit(solution)/shard_map/ppermute | solution.py:235
  7.4 15.4 %collective-permute-start.1 = (bf16[256,128]{1,0:T(8,128)(2,1)S(1)}, bf16[256,128]{1,0:T(8,128)(2,1)S(1)}, u32[]{:S(2)}, u32[]{:S(2)}) collective-permute-start(bf16[256,128]{1,0:T(8,128)(2,1)S(1)} %get-tuple-element.27), channel_id=1, source_target_pairs={{0,16},{2,18},{16,0},{18,2},{1,17},{3,19},{17,1},{19,3},{4,20},{6,... | collective-permute-start | bytes 196616 | tf_op jit(solution)/shard_map/ppermute | solution.py:235
  7.8 15.1 %collective-permute-start = (bf16[384,128]{1,0:T(8,128)(2,1)S(1)}, bf16[384,128]{1,0:T(8,128)(2,1)S(1)}, u32[]{:S(2)}, u32[]{:S(2)}) collective-permute-start(bf16[384,128]{1,0:T(8,128)(2,1)S(1)} %get-tuple-element.26), channel_id=1, source_target_pairs={{0,2},{2,0},{16,18},{18,16},{1,3},{3,1},{17,19},{19,17},{4,6},{6,4... | collective-permute-start | bytes 294920 | tf_op jit(solution)/shard_map/ppermute | solution.py:235
  12.0 22.0 %all-to-all-start = ((bf16[16,8,1024]{2,1,0:T(8,128)(2,1)}), bf16[16,8,1024]{2,1,0:T(8,128)(2,1)S(1)}, u32[]{:S(2)}, u32[]{:S(2)}) async-start(bf16[16,8,1024]{2,1,0:T(8,128)(2,1)} %bitcast.23), calls=%async_computation | async-start | bytes 524288 | tf_op jit(solution)/shard_map/all_to_all | solution.py:30
  23.0 13.2 %copy-start.7 = (bf16[1280,128]{1,0:T(8,128)(2,1)}, bf16[1280,128]{1,0:T(8,128)(2,1)S(1)}, u32[]{:S(2)}) copy-start(bf16[1280,128]{1,0:T(8,128)(2,1)S(1)} %slice_dynamic-update-slice_fusion.2.refs_0_.kv0_ref) | copy-start | bytes 983044
  23.0 19.3 %collective-permute-start.5 = (bf16[1280,128]{1,0:T(8,128)(2,1)S(1)}, bf16[1280,128]{1,0:T(8,128)(2,1)S(1)}, u32[]{:S(2)}, u32[]{:S(2)}) collective-permute-start(bf16[1280,128]{1,0:T(8,128)(2,1)S(1)} %slice_dynamic-update-slice_fusion.2.refs_0_.kv0_ref), channel_id=1, source_target_pairs={{0,12},{4,0},{8,4},{12,8},{1,13},{5,1},{9,5},{13,9},{2,14},{6,2},{... | collective-permute-start | bytes 983048 | tf_op jit(solution)/shard_map/ppermute | solution.py:231
  25.5 16.8 %collective-permute-start.4 = (bf16[1280,128]{1,0:T(8,128)(2,1)S(1)}, bf16[1280,128]{1,0:T(8,128)(2,1)S(1)}, u32[]{:S(2)}, u32[]{:S(2)}) collective-permute-start(bf16[1280,128]{1,0:T(8,128)(2,1)S(1)} %slice_dynamic-update-slice_fusion.2.refs_0_.kv0_ref), channel_id=1, source_target_pairs={{0,8},{4,12},{8,0},{12,4},{1,9},{5,13},{9,1},{13,5},{2,10},{6,14},... | collective-permute-start | bytes 983048 | tf_op jit(solution)/shard_map/ppermute | solution.py:231
  26.0 17.6 %collective-permute-start.3 = (bf16[1280,128]{1,0:T(8,128)(2,1)S(1)}, bf16[1280,128]{1,0:T(8,128)(2,1)S(1)}, u32[]{:S(2)}, u32[]{:S(2)}) collective-permute-start(bf16[1280,128]{1,0:T(8,128)(2,1)S(1)} %slice_dynamic-update-slice_fusion.2.refs_0_.kv0_ref), channel_id=1, source_target_pairs={{0,4},{4,8},{8,12},{12,0},{1,5},{5,9},{9,13},{13,1},{2,6},{6,10},{... | collective-permute-start | bytes 983048 | tf_op jit(solution)/shard_map/ppermute | solution.py:231
  36.2 24.0 %all-to-all-start.1 = ((bf16[8,48,1024]{2,1,0:T(8,128)(2,1)}), bf16[8,48,1024]{2,1,0:T(8,128)(2,1)S(1)}, u32[]{:S(2)}, u32[]{:S(2)}) async-start(bf16[8,48,1024]{2,1,0:T(8,128)(2,1)} %shard_map.129), calls=%async_computation.1 | async-start | bytes 1572864 | tf_op jit(solution)/shard_map/all_to_all | solution.py:30
  42.3 17.9 %copy-start.8 = (bf16[1280,128]{1,0:T(8,128)(2,1)}, bf16[1280,128]{1,0:T(8,128)(2,1)S(1)}, u32[]{:S(2)}) copy-start(bf16[1280,128]{1,0:T(8,128)(2,1)S(1)} %collective-permute-done.5.refs_3_.kv3_ref) | copy-start | bytes 983044
  42.3 17.9 %copy-start.9 = (bf16[1280,128]{1,0:T(8,128)(2,1)}, bf16[1280,128]{1,0:T(8,128)(2,1)S(1)}, u32[]{:S(2)}) copy-start(bf16[1280,128]{1,0:T(8,128)(2,1)S(1)} %collective-permute-done.4.refs_2_.kv2_ref) | copy-start | bytes 983044
  43.7 16.5 %copy-start.10 = (bf16[1280,128]{1,0:T(8,128)(2,1)}, bf16[1280,128]{1,0:T(8,128)(2,1)S(1)}, u32[]{:S(2)}) copy-start(bf16[1280,128]{1,0:T(8,128)(2,1)S(1)} %collective-permute-done.3.refs_1_.kv1_ref) | copy-start | bytes 983044
  60.1 0.9 copy-start.6
  75.9 8.1 %copy-start.13 = (bf16[1024,128]{1,0:T(8,128)(2,1)S(1)}, bf16[1024,128]{1,0:T(8,128)(2,1)}, u32[]{:S(2)}) copy-start(bf16[1024,128]{1,0:T(8,128)(2,1)} %get-tuple-element.30) | copy-start | bytes 786436
  75.9 10.0 %copy-start.12 = (bf16[1024,128]{1,0:T(8,128)(2,1)S(1)}, bf16[1024,128]{1,0:T(8,128)(2,1)}, u32[]{:S(2)}) copy-start(bf16[1024,128]{1,0:T(8,128)(2,1)} %get-tuple-element.31) | copy-start | bytes 786436
  75.9 10.6 %copy-start.11 = (bf16[1024,128]{1,0:T(8,128)(2,1)S(1)}, bf16[1024,128]{1,0:T(8,128)(2,1)}, u32[]{:S(2)}) copy-start(bf16[1024,128]{1,0:T(8,128)(2,1)} %get-tuple-element.32) | copy-start | bytes 786436
  75.9 43.5 %all-to-all-start.2 = ((bf16[128,8,512]{2,1,0:T(8,128)(2,1)}), bf16[128,8,512]{2,1,0:T(8,128)(2,1)S(1)}, u32[]{:S(2)}, u32[]{:S(2)}) async-start(bf16[128,8,512]{2,1,0:T(8,128)(2,1)} %get-tuple-element.28), calls=%async_computation.2 | async-start | bytes 2097152 | tf_op jit(solution)/shard_map/all_to_all | solution.py:30
  84.1 12.6 %collective-permute-start.6 = (bf16[1024,128]{1,0:T(8,128)(2,1)S(1)}, bf16[1024,128]{1,0:T(8,128)(2,1)S(1)}, u32[]{:S(2)}, u32[]{:S(2)}) collective-permute-start(bf16[1024,128]{1,0:T(8,128)(2,1)S(1)} %copy-done.13), channel_id=1, source_target_pairs={{0,12},{4,0},{8,4},{12,8},{1,13},{5,1},{9,5},{13,9},{2,14},{6,2},{... | collective-permute-start | bytes 786440 | tf_op jit(solution)/shard_map/ppermute | solution.py:231
  85.9 12.5 %collective-permute-start.7 = (bf16[1024,128]{1,0:T(8,128)(2,1)S(1)}, bf16[1024,128]{1,0:T(8,128)(2,1)S(1)}, u32[]{:S(2)}, u32[]{:S(2)}) collective-permute-start(bf16[1024,128]{1,0:T(8,128)(2,1)S(1)} %copy-done.12), channel_id=1, source_target_pairs={{0,8},{4,12},{8,0},{12,4},{1,9},{5,13},{9,1},{13,5},{2,10},{6,14},... | collective-permute-start | bytes 786440 | tf_op jit(solution)/shard_map/ppermute | solution.py:231
  86.5 23.5 %copy-start = (bf16[1024,128]{1,0:T(8,128)(2,1)S(1)}, bf16[1024,128]{1,0:T(8,128)(2,1)}, u32[]{:S(2)}) copy-start(bf16[1024,128]{1,0:T(8,128)(2,1)} %get-tuple-element.35.a_ref) | copy-start | bytes 786436
  86.5 23.5 %collective-permute-start.8 = (bf16[1024,128]{1,0:T(8,128)(2,1)S(1)}, bf16[1024,128]{1,0:T(8,128)(2,1)S(1)}, u32[]{:S(2)}, u32[]{:S(2)}) collective-permute-start(bf16[1024,128]{1,0:T(8,128)(2,1)S(1)} %copy-done.11), channel_id=1, source_target_pairs={{0,4},{4,8},{8,12},{12,0},{1,5},{5,9},{9,13},{13,1},{2,6},{6,10},{... | collective-permute-start | bytes 786440 | tf_op jit(solution)/shard_map/ppermute | solution.py:231
  110.1 9.3 %copy-start.1 = (f32[32,1792]{1,0:T(8,128)S(1)}, f32[32,1792]{1,0:T(8,128)}, u32[]{:S(2)}) copy-start(f32[32,1792]{1,0:T(8,128)} %get-tuple-element.34.own_ref) | copy-start | bytes 688132
  110.1 4.2 %collective-permute-start.9 = (bf16[256,128]{1,0:T(8,128)(2,1)S(1)}, bf16[256,128]{1,0:T(8,128)(2,1)S(1)}, u32[]{:S(2)}, u32[]{:S(2)}) collective-permute-start(bf16[256,128]{1,0:T(8,128)(2,1)S(1)} %get-tuple-element.40), channel_id=1, source_target_pairs={{0,2},{2,0},{16,18},{18,16},{1,3},{3,1},{17,19},{19,17},{4,6},{6,4... | collective-permute-start | bytes 196616 | tf_op jit(solution)/shard_map/ppermute | solution.py:235
  111.4 5.7 %collective-permute-start.10 = (bf16[256,128]{1,0:T(8,128)(2,1)S(1)}, bf16[256,128]{1,0:T(8,128)(2,1)S(1)}, u32[]{:S(2)}, u32[]{:S(2)}) collective-permute-start(bf16[256,128]{1,0:T(8,128)(2,1)S(1)} %get-tuple-element.41), channel_id=1, source_target_pairs={{0,16},{2,18},{16,0},{18,2},{1,17},{3,19},{17,1},{19,3},{4,20},{6,... | collective-permute-start | bytes 196616 | tf_op jit(solution)/shard_map/ppermute | solution.py:235
  114.3 4.5 %collective-permute-start.11 = (bf16[256,128]{1,0:T(8,128)(2,1)S(1)}, bf16[256,128]{1,0:T(8,128)(2,1)S(1)}, u32[]{:S(2)}, u32[]{:S(2)}) collective-permute-start(bf16[256,128]{1,0:T(8,128)(2,1)S(1)} %get-tuple-element.42), channel_id=1, source_target_pairs={{0,18},{2,16},{16,2},{18,0},{1,19},{3,17},{17,3},{19,1},{4,22},{6,... | collective-permute-start | bytes 196616 | tf_op jit(solution)/shard_map/ppermute | solution.py:235

commit v2 on v1

--- a/solution.py
+++ b/solution.py
@@ -19,6 +19,7 @@
 LIVE = 144
 STATS = GROUP * HEAD_WIDTH
 INTERPRET = False
+KEY_BLOCK, ROW_BLOCK = 512, 512
 VMEM_BYTES = 24 * 1024 * 1024
 BF16 = jnp.bfloat16
 F32 = jnp.float32
@@ -123,37 +124,34 @@
     q_scr[GROUP * LIVE :, :] = jnp.zeros((1024 - GROUP * LIVE, 2 * HEAD_WIDTH), BF16)
     g_scr[GROUP * LIVE :, :] = jnp.zeros((1024 - GROUP * LIVE, 2 * HEAD_WIDTH), BF16)
 
-    lane = lax.broadcasted_iota(jnp.int32, (256, HEAD_WIDTH), 1)
+    lane = lax.broadcasted_iota(jnp.int32, (KEY_BLOCK, HEAD_WIDTH), 1)
     minus = jnp.where(lane < 6 * GROUP, -1.0, 0.0).astype(BF16)
-
-    def block(kv_ref, kvg_ref, pair):
-        def piece(k):
-            return pl.ds(pl.multiple_of(pair * 512 + k * 128, 128), 128)
-
-        keys = jnp.concatenate([kv_ref[piece(0), :], kv_ref[piece(2), :]], axis=0)
-        values = jnp.concatenate([kv_ref[piece(1), :], kv_ref[piece(3), :]], axis=0)
-        wide_keys = jnp.concatenate([keys, minus], axis=1)
-        wide_values = jnp.concatenate([values, minus], axis=1)
-        gk = jnp.zeros(keys.shape, F32)
-        gv = jnp.zeros(keys.shape, F32)
-        for part in range(4):
-            rows = slice(256 * part, 256 * part + 256)
-            prob = jnp.exp(dot(wide_keys, q_scr[rows, :], 1, 1) * SCALE)
-            sgrad = (prob * dot(wide_values, g_scr[rows, :], 1, 1)).astype(BF16)
-            gv = gv + dot(prob.astype(BF16), g_scr[rows, 0:HEAD_WIDTH], 1, 0)
-            gk = gk + dot(sgrad, q_scr[rows, 0:HEAD_WIDTH], 1, 0)
-            acc_ref[rows, :] += dot(sgrad, keys, 0, 0)
-        gk, gv = (gk * SCALE).astype(BF16), gv.astype(BF16)
-        for k, part in enumerate((gk[0:128], gv[0:128], gk[128:256], gv[128:256])):
-            kvg_ref[piece(k), :] = part
-
     for kv_ref, kvg_ref in zip(kv_refs, kvg_refs):
-        lax.fori_loop(0, 2, lambda k, _: block(kv_ref, kvg_ref, k), None)
+        for first in range(0, 1024, 2 * KEY_BLOCK):
+            starts = range(first, first + 2 * KEY_BLOCK, 256)
+            keys = jnp.concatenate([kv_ref[k : k + 128, :] for k in starts], axis=0)
+            values = jnp.concatenate([kv_ref[k + 128 : k + 256, :] for k in starts], axis=0)
+            turned = keys.T
+            wide_keys = jnp.concatenate([keys, minus], axis=1)
+            wide_values = jnp.concatenate([values, minus], axis=1)
+            gk = jnp.zeros(keys.shape, F32)
+            gv = jnp.zeros(keys.shape, F32)
+            for part in range(0, 1024, ROW_BLOCK):
+                rows = slice(part, part + ROW_BLOCK)
+                prob = jnp.exp2(dot(wide_keys, q_scr[rows, :], 1, 1) * (SCALE / math.log(2)))
+                sgrad = (prob * dot(wide_values, g_scr[rows, :], 1, 1)).astype(BF16)
+                gv = gv + dot(prob.astype(BF16), g_scr[rows, 0:HEAD_WIDTH], 1, 0)
+                gk = gk + dot(sgrad, q_scr[rows, 0:HEAD_WIDTH], 1, 0)
+                acc_ref[:, rows] += dot(turned, sgrad, 1, 0)
+            for n, k in enumerate(starts):
+                kvg_ref[k : k + 128, :] = (gk[128 * n : 128 * n + 128] * SCALE).astype(BF16)
+                kvg_ref[k + 128 : k + 256, :] = gv[128 * n : 128 * n + 128].astype(BF16)
 
     back_ref[...] = jnp.zeros_like(back_ref)
+    sums = acc_ref[...].T
     for head in range(GROUP):
         lanes = slice(head % 4 * HEAD_WIDTH, (head % 4 + 1) * HEAD_WIDTH)
-        part = (acc_ref[head * LIVE : (head + 1) * LIVE, :] * SCALE).astype(BF16)
+        part = (sums[head * LIVE : (head + 1) * LIVE, :] * SCALE).astype(BF16)
         back_ref[head // 4 * LIVE : (head // 4 + 1) * LIVE, lanes] = part
     slot = out_slot_ref[0:1, :]
     hit = lax.broadcasted_iota(jnp.int32, (2 * LIVE, slot.shape[1]), 0) == slot
@@ -164,17 +162,16 @@
 def prompt_terms(in_slot, out_slot, rows, *kv):
     *kv_grads, gq = call(
         prompt_kernel,
-        [jax.ShapeDtypeStruct((1024, HEAD_WIDTH), BF16)] * 4
-        + [jax.ShapeDtypeStruct((128, 8, 512), BF16)],
+        [pltpu.HBM((1024, HEAD_WIDTH), BF16)] * 4 + [pltpu.HBM((128, 8, 512), BF16)],
         in_slot,
         out_slot,
         rows,
         *kv,
-        small=False,
+        out_specs=[pl.BlockSpec(memory_space=pltpu.VMEM)] * 5,
         scratch_shapes=[
             pltpu.VMEM((1024, 2 * HEAD_WIDTH), BF16),
             pltpu.VMEM((1024, 2 * HEAD_WIDTH), BF16),
-            pltpu.VMEM((1024, HEAD_WIDTH), F32),
+            pltpu.VMEM((HEAD_WIDTH, 1024), F32),
             pltpu.VMEM((2 * LIVE, 512), BF16),
         ],
     )
@@ -206,6 +203,13 @@
         other_ref[rows, :] = jnp.where(half == 0, ref[:, high], ref[:, low])
     for k, (ref, lanes) in enumerate(((sk_ref, low), (sk_ref, high), (sv_ref, low), (sv_ref, high))):
         own_ref[256 + 32 * k : 288 + 32 * k, :] = ref[:, lanes]
+
+
+def join_kernel(own_ref, beside_ref, third_ref, fourth_ref, out_ref):
+    for k, ref in enumerate((own_ref, beside_ref, third_ref, fourth_ref)):
+        out_ref[256 * k : 256 * k + 256, :] = ref[0:256, :]
+    out_ref[1024:1152, :] = own_ref[256:384, :]
+    out_ref[1152:1280, :] = beside_ref[256:384, :]
 
 
 def x_sum_kernel(a_ref, b_ref, c_ref, d_ref, *out_refs):
@@ -343,10 +347,8 @@
         slice_value_rows[0],
         in_specs=[smem] + [vmem] * 4,
     )
-    beside = crossed(own, 1)
-    column = jnp.concatenate(
-        [own[:256], beside[:256], crossed(other, 2), crossed(other, 3), own[256:], beside[256:]]
-    )
+    around = [own, crossed(own, 1), crossed(other, 2), crossed(other, 3)]
+    column = call(join_kernel, packed(1280), *around)
     kv = [column] + [shifted(column, k) for k in (1, 2, 3)]
 
     all_lengths = arrived[:, 0, STATS + 6 * GROUP].astype(jnp.int32)

time: 121 us -> 111 us (0.917)
  the two profiles are of different devices: /device:TPU:1 before, /device:TPU:8 now
where the time goes in v2:
time: 111 us; the launch traced here: 109 us
  starting transfers between devices  42.9 us (39%)
  waiting for transfers between devices  39.1 us (35%)
  Pallas kernels  23.7 us (21%)
  other arithmetic  1.6 us (1%)
  between operations  1.52 us (1%)
    pallas_call x9, Pallas kernels, call(): pl.pallas_call(body, out_shape=out_shape, interpret=INTERPRET, compiler_p...  23.7 us
    all_to_all x3, starting transfers between devices, exchange(): return lax.all_to_all(tiles, axes, split_axis=0, concat_axis=0, tiled=True)  23 us
    all_to_all x3, waiting for transfers between devices, exchange(): return lax.all_to_all(tiles, axes, split_axis=0, concat_axis=0, tiled=True)  18.2 us
    ppermute x6, waiting for transfers between devices, shifted(): return lax.ppermute(value, ALONG_X, [(k, (k + by) % 4) for k in range(4)])  13.2 us
    ppermute x6, starting transfers between devices, shifted(): return lax.ppermute(value, ALONG_X, [(k, (k + by) % 4) for k in range(4)])  10.2 us
    ppermute x6, starting transfers between devices, crossed(): return lax.ppermute(value, ALONG_Y, [(k, k ^ by) for k in range(4)])  9.65 us
    ppermute x6, waiting for transfers between devices, crossed(): return lax.ppermute(value, ALONG_Y, [(k, k ^ by) for k in range(4)])  7.74 us
  transfers between devices with their start and end apart: 15, of which 10 were waited for; matrix products, arithmetic and copies ran while one was open for 2% of the time, Pallas kernels for 11%

profile of v2, /device:TPU:8, one launch (start us, length us, event | category | flops | bytes accessed | tf_op | source)
XLA Modules:
  0.0 109.3 jit_solution(4266994717310679921)
XLA Ops:
  1.3 3.2 %shard_map.128 = bf16[8,2,8,1024]{3,2,1,0:T(8,128)(2,1)} custom-call(s32[1]{0:T(128)} %bitcast.p_ref, s32[1]{0:T(128)} %bitcast.1.turn_ref, s32[1]{0:T(128)S(6)} %copy.17.live_ref, bf16[256,1792]{1,0:T(8,128)(2,1)} %bitcast.17, bf16[256,1792]{1,0:T(8,128)(2,1)} %bitcast.19, bf16[256,1792]{1,0:T(8,128)(2,1)} %bitcast.21, f32[14,1,256]{2,1,0:T(1,128)} %bitcast.26), custom_call_target="tpu_custom_call" | custom-call | tf_op jit(solution)/shard_map/pallas_call | solution.py:40
  4.5 10.4 %all-to-all-start = ((bf16[16,8,1024]{2,1,0:T(8,128)(2,1)}), bf16[16,8,1024]{2,1,0:T(8,128)(2,1)S(1)}, u32[]{:S(2)}, u32[]{:S(2)}) async-start(bf16[16,8,1024]{2,1,0:T(8,128)(2,1)} %bitcast.23), calls=%async_computation | async-start | bytes 524288 | tf_op jit(solution)/shard_map/all_to_all | solution.py:31
  15.1 3.5 %collective-permute-start.1 = (bf16[256,128]{1,0:T(8,128)(2,1)S(1)}, bf16[256,128]{1,0:T(8,128)(2,1)S(1)}, u32[]{:S(2)}, u32[]{:S(2)}) collective-permute-start(bf16[256,128]{1,0:T(8,128)(2,1)S(1)} %get-tuple-element.27), channel_id=1, source_target_pairs={{0,16},{2,18},{16,0},{18,2},{1,17},{3,19},{17,1},{19,3},{4,20},{6,... | collective-permute-start | bytes 196616 | tf_op jit(solution)/shard_map/ppermute | solution.py:239
  18.6 1.3 %collective-permute-start = (bf16[384,128]{1,0:T(8,128)(2,1)S(1)}, bf16[384,128]{1,0:T(8,128)(2,1)S(1)}, u32[]{:S(2)}, u32[]{:S(2)}) collective-permute-start(bf16[384,128]{1,0:T(8,128)(2,1)S(1)} %get-tuple-element.26.own_ref), channel_id=1, source_target_pairs={{0,2},{2,0},{16,18},{18,16},{1,3},{3,1},{17,19},{19,17},{4,6},{6,4... | collective-permute-start | bytes 294920 | tf_op jit(solution)/shard_map/ppermute | solution.py:239
  20.0 1.5 %collective-permute-done.1.third_ref = bf16[256,128]{1,0:T(8,128)(2,1)S(1)} collective-permute-done((bf16[256,128]{1,0:T(8,128)(2,1)S(1)}, bf16[256,128]{1,0:T(8,128)(2,1)S(1)}, u32[]{:S(2)}, u32[]{:S(2)}) %collective-permute-start.1) | collective-permute-done | bytes 65568 | tf_op jit(solution)/shard_map/ppermute | solution.py:239
  21.5 2.0 %collective-permute-done.2.fourth_ref = bf16[256,128]{1,0:T(8,128)(2,1)S(1)} collective-permute-done((bf16[256,128]{1,0:T(8,128)(2,1)S(1)}, bf16[256,128]{1,0:T(8,128)(2,1)S(1)}, u32[]{:S(2)}, u32[]{:S(2)}) %collective-permute-start.2) | collective-permute-done | bytes 65568 | tf_op jit(solution)/shard_map/ppermute | solution.py:239
  23.6 1.9 %collective-permute-done.beside_ref = bf16[384,128]{1,0:T(8,128)(2,1)S(1)} collective-permute-done((bf16[384,128]{1,0:T(8,128)(2,1)S(1)}, bf16[384,128]{1,0:T(8,128)(2,1)S(1)}, u32[]{:S(2)}, u32[]{:S(2)}) %collective-permute-start) | collective-permute-done | bytes 98336 | tf_op jit(solution)/shard_map/ppermute | solution.py:239
  25.5 1.6 %collective-permute-start.3 = (bf16[1280,128]{1,0:T(8,128)(2,1)S(1)}, bf16[1280,128]{1,0:T(8,128)(2,1)S(1)}, u32[]{:S(2)}, u32[]{:S(2)}) collective-permute-start(bf16[1280,128]{1,0:T(8,128)(2,1)S(1)} %shard_map.131.refs_0_.kv0_ref), channel_id=1, source_target_pairs={{0,4},{4,8},{8,12},{12,0},{1,5},{5,9},{9,13},{13,1},{2,6},{6,10},{... | collective-permute-start | bytes 983048 | tf_op jit(solution)/shard_map/ppermute | solution.py:235
  27.0 2.7 %collective-permute-start.4 = (bf16[1280,128]{1,0:T(8,128)(2,1)S(1)}, bf16[1280,128]{1,0:T(8,128)(2,1)S(1)}, u32[]{:S(2)}, u32[]{:S(2)}) collective-permute-start(bf16[1280,128]{1,0:T(8,128)(2,1)S(1)} %shard_map.131.refs_0_.kv0_ref), channel_id=1, source_target_pairs={{0,8},{4,12},{8,0},{12,4},{1,9},{5,13},{9,1},{13,5},{2,10},{6,14},... | collective-permute-start | bytes 983048 | tf_op jit(solution)/shard_map/ppermute | solution.py:235
  29.8 1.4 %collective-permute-start.5 = (bf16[1280,128]{1,0:T(8,128)(2,1)S(1)}, bf16[1280,128]{1,0:T(8,128)(2,1)S(1)}, u32[]{:S(2)}, u32[]{:S(2)}) collective-permute-start(bf16[1280,128]{1,0:T(8,128)(2,1)S(1)} %shard_map.131.refs_0_.kv0_ref), channel_id=1, source_target_pairs={{0,12},{4,0},{8,4},{12,8},{1,13},{5,1},{9,5},{13,9},{2,14},{6,2},{... | collective-permute-start | bytes 983048 | tf_op jit(solution)/shard_map/ppermute | solution.py:235
  31.2 0.0 all-to-all-done.rows_ref
  31.2 1.4 %shard_map.129 = bf16[8,48,1024]{2,1,0:T(8,128)(2,1)} custom-call(s32[1]{0:T(128)} %bitcast.p_ref, s32[1]{0:T(128)} %bitcast.8.z_ref, bf16[16,8,1024]{2,1,0:T(8,128)(2,1)S(1)} %all-to-all-done.rows_ref), custom_call_target="tpu_custom_call" | custom-call | tf_op jit(solution)/shard_map/pallas_call | solution.py:40
  32.6 6.5 %all-to-all-start.1 = ((bf16[8,48,1024]{2,1,0:T(8,128)(2,1)}), bf16[8,48,1024]{2,1,0:T(8,128)(2,1)S(1)}, u32[]{:S(2)}, u32[]{:S(2)}) async-start(bf16[8,48,1024]{2,1,0:T(8,128)(2,1)} %shard_map.129), calls=%async_computation.1 | async-start | bytes 1572864 | tf_op jit(solution)/shard_map/all_to_all | solution.py:31
  39.1 0.4 fusion.5
  39.6 0.1 fusion.11
  39.7 0.1 select_reduce_fusion.2
  39.9 0.4 select_reduce_fusion.1
  40.2 0.1 select_reduce_fusion
  40.3 0.1 copy.15
  40.4 0.1 add_select_fusion
  40.5 0.1 copy.16
  40.6 0.1 iota_add_fusion
  40.7 0.1 broadcast_add_fusion
  40.8 0.1 iota_compare_fusion.3
  40.9 0.2 add.190.out_slot_ref
  41.1 0.1 add_select_fusion.2
  41.1 0.1 select_n.95.in_slot_ref
  41.3 0.0 collective-permute-done.3.refs_1_.kv1_ref
  41.3 1.8 %collective-permute-done.4.refs_2_.kv2_ref = bf16[1280,128]{1,0:T(8,128)(2,1)S(1)} collective-permute-done((bf16[1280,128]{1,0:T(8,128)(2,1)S(1)}, bf16[1280,128]{1,0:T(8,128)(2,1)S(1)}, u32[]{:S(2)}, u32[]{:S(2)}) %collective-permute-start.4) | collective-permute-done | bytes 327712 | tf_op jit(solution)/shard_map/ppermute | solution.py:235
  43.1 0.0 collective-permute-done.5.refs_3_.kv3_ref
  43.1 18.2 %all-to-all-done.1.rows_ref = bf16[8,48,1024]{2,1,0:T(8,128)(2,1)S(1)} async-done(((bf16[8,48,1024]{2,1,0:T(8,128)(2,1)}), bf16[8,48,1024]{2,1,0:T(8,128)(2,1)S(1)}, u32[]{:S(2)}, u32[]{:S(2)}) %all-to-all-start.1) | async-done | bytes 786464 | tf_op jit(solution)/shard_map/all_to_all | solution.py:31
  61.3 8.0 %shard_map.132 = (bf16[1024,128]{1,0:T(8,128)(2,1)}, bf16[1024,128]{1,0:T(8,128)(2,1)}, bf16[1024,128]{1,0:T(8,128)(2,1)}, bf16[1024,128]{1,0:T(8,128)(2,1)}, bf16[128,8,512]{2,1,0:T(8,128)(2,1)}) custom-call(s32[1,384]{1,0:T(1,128)S(1)} %select_n.95.in_slot_ref, s32[1,1024]{1,0:T(1,128)S(1)} %add.190.out_slot_ref, ...), custom_call_target="tpu_custom_call" | custom-call | tf_op jit(solution)/shard_map/pallas_call | solution.py:40
  69.3 6.1 %all-to-all-start.2 = ((bf16[128,8,512]{2,1,0:T(8,128)(2,1)}), bf16[128,8,512]{2,1,0:T(8,128)(2,1)S(1)}, u32[]{:S(2)}, u32[]{:S(2)}) async-start(bf16[128,8,512]{2,1,0:T(8,128)(2,1)} %get-tuple-element.28), calls=%async_computation.2 | async-start | bytes 2097152 | tf_op jit(solution)/shard_map/all_to_all | solution.py:31
  75.3 2.8 %collective-permute-start.6 = (bf16[1024,128]{1,0:T(8,128)(2,1)S(1)}, bf16[1024,128]{1,0:T(8,128)(2,1)S(1)}, u32[]{:S(2)}, u32[]{:S(2)}) collective-permute-start(bf16[1024,128]{1,0:T(8,128)(2,1)S(1)} %copy-done.12), channel_id=1, source_target_pairs={{0,12},{4,0},{8,4},{12,8},{1,13},{5,1},{9,5},{13,9},{2,14},{6,2},{... | collective-permute-start | bytes 786440 | tf_op jit(solution)/shard_map/ppermute | solution.py:235
  78.1 0.8 collective-permute-start.7
  79.0 0.9 collective-permute-start.8
  79.9 9.4 %shard_map.133 = (bf16[32,256]{1,0:T(8,128)(2,1)}, bf16[32,256]{1,0:T(8,128)(2,1)}, f32[32,1792]{1,0:T(8,128)}) custom-call(s32[1]{0:T(128)} %bitcast.p_ref, s32[1]{0:T(128)S(6)} %copy.17.live_ref, bf16[256,1792]{1,0:T(8,128)(2,1)} %bitcast.18, bf16[256,1792]{1,0:T(8,128)(2,1)} %bitcast.20, bf16[256,1792]{1,0:T(8,128)(2,1)} %bitcast.22, ...), custom_call_target="tpu_custom_call" | custom-call | tf_op jit(solution)/shard_map/pallas_call | solution.py:40
  89.3 8.6 %collective-permute-done.6.b_ref = bf16[1024,128]{1,0:T(8,128)(2,1)S(1)} collective-permute-done((bf16[1024,128]{1,0:T(8,128)(2,1)S(1)}, bf16[1024,128]{1,0:T(8,128)(2,1)S(1)}, u32[]{:S(2)}, u32[]{:S(2)}) %collective-permute-start.6) | collective-permute-done | bytes 262176 | tf_op jit(solution)/shard_map/ppermute | solution.py:235
  97.9 0.0 collective-permute-done.7.c_ref
  97.9 2.8 %collective-permute-done.8.d_ref = bf16[1024,128]{1,0:T(8,128)(2,1)S(1)} collective-permute-done((bf16[1024,128]{1,0:T(8,128)(2,1)S(1)}, bf16[1024,128]{1,0:T(8,128)(2,1)S(1)}, u32[]{:S(2)}, u32[]{:S(2)}) %collective-permute-start.8) | collective-permute-done | bytes 262176 | tf_op jit(solution)/shard_map/ppermute | solution.py:235
  100.6 0.1 shard_map.135
  100.8 2.5 %collective-permute-start.10 = (bf16[256,128]{1,0:T(8,128)(2,1)S(1)}, bf16[256,128]{1,0:T(8,128)(2,1)S(1)}, u32[]{:S(2)}, u32[]{:S(2)}) collective-permute-start(bf16[256,128]{1,0:T(8,128)(2,1)S(1)} %get-tuple-element.41), channel_id=1, source_target_pairs={{0,16},{2,18},{16,0},{18,2},{1,17},{3,19},{17,1},{19,3},{4,20},{6,... | collective-permute-start | bytes 196616 | tf_op jit(solution)/shard_map/ppermute | solution.py:239
  103.3 2.3 %collective-permute-start.9 = (bf16[256,128]{1,0:T(8,128)(2,1)S(1)}, bf16[256,128]{1,0:T(8,128)(2,1)S(1)}, u32[]{:S(2)}, u32[]{:S(2)}) collective-permute-start(bf16[256,128]{1,0:T(8,128)(2,1)S(1)} %get-tuple-element.40), channel_id=1, source_target_pairs={{0,2},{2,0},{16,18},{18,16},{1,3},{3,1},{17,19},{19,17},{4,6},{6,4... | collective-permute-start | bytes 196616 | tf_op jit(solution)/shard_map/ppermute | solution.py:239
  105.6 1.2 %collective-permute-done.10.c_ref = bf16[256,128]{1,0:T(8,128)(2,1)S(1)} collective-permute-done((bf16[256,128]{1,0:T(8,128)(2,1)S(1)}, bf16[256,128]{1,0:T(8,128)(2,1)S(1)}, u32[]{:S(2)}, u32[]{:S(2)}) %collective-permute-start.10) | collective-permute-done | bytes 65568 | tf_op jit(solution)/shard_map/ppermute | solution.py:239
  106.7 1.0 collective-permute-done.11.d_ref
  107.8 0.1 collective-permute-done.9.b_ref
  107.9 0.7 shard_map.136
  108.5 0.8 shard_map.134
  (37 shorter events, 0.2 us)
Async XLA Ops:
  4.5 10.5 %copy-start.6 = (bf16[128,256]{1,0:T(8,128)(2,1)S(1)}, bf16[128,256]{1,0:T(8,128)(2,1)}, u32[]{:S(2)}) copy-start(bf16[128,256]{1,0:T(8,128)(2,1)} %pk_ref.1) | copy-start | bytes 196612
  4.5 10.5 %copy-start.7 = (bf16[128,256]{1,0:T(8,128)(2,1)S(1)}, bf16[128,256]{1,0:T(8,128)(2,1)}, u32[]{:S(2)}) copy-start(bf16[128,256]{1,0:T(8,128)(2,1)} %pv_ref.1) | copy-start | bytes 196612
  4.5 10.5 %copy-start.8 = (bf16[1,32,256]{2,1,0:T(8,128)(2,1)S(1)}, bf16[1,32,256]{2,1,0:T(8,128)(2,1)}, u32[]{:S(2)}) copy-start(bf16[1,32,256]{2,1,0:T(8,128)(2,1)} %param.16) | copy-start | bytes 49156
  4.5 10.5 %copy-start.9 = (bf16[1,32,256]{2,1,0:T(8,128)(2,1)S(1)}, bf16[1,32,256]{2,1,0:T(8,128)(2,1)}, u32[]{:S(2)}) copy-start(bf16[1,32,256]{2,1,0:T(8,128)(2,1)} %param.17) | copy-start | bytes 49156
  4.5 26.7 %all-to-all-start = ((bf16[16,8,1024]{2,1,0:T(8,128)(2,1)}), bf16[16,8,1024]{2,1,0:T(8,128)(2,1)S(1)}, u32[]{:S(2)}, u32[]{:S(2)}) async-start(bf16[16,8,1024]{2,1,0:T(8,128)(2,1)} %bitcast.23), calls=%async_computation | async-start | bytes 524288 | tf_op jit(solution)/shard_map/all_to_all | solution.py:31
  15.1 6.4 %collective-permute-start.1 = (bf16[256,128]{1,0:T(8,128)(2,1)S(1)}, bf16[256,128]{1,0:T(8,128)(2,1)S(1)}, u32[]{:S(2)}, u32[]{:S(2)}) collective-permute-start(bf16[256,128]{1,0:T(8,128)(2,1)S(1)} %get-tuple-element.27), channel_id=1, source_target_pairs={{0,16},{2,18},{16,0},{18,2},{1,17},{3,19},{17,1},{19,3},{4,20},{6,... | collective-permute-start | bytes 196616 | tf_op jit(solution)/shard_map/ppermute | solution.py:239
  18.6 5.0 %collective-permute-start.2 = (bf16[256,128]{1,0:T(8,128)(2,1)S(1)}, bf16[256,128]{1,0:T(8,128)(2,1)S(1)}, u32[]{:S(2)}, u32[]{:S(2)}) collective-permute-start(bf16[256,128]{1,0:T(8,128)(2,1)S(1)} %get-tuple-element.27), channel_id=1, source_target_pairs={{0,18},{2,16},{16,2},{18,0},{1,19},{3,17},{17,3},{19,1},{4,22},{6,... | collective-permute-start | bytes 196616 | tf_op jit(solution)/shard_map/ppermute | solution.py:239
  18.6 6.8 %collective-permute-start = (bf16[384,128]{1,0:T(8,128)(2,1)S(1)}, bf16[384,128]{1,0:T(8,128)(2,1)S(1)}, u32[]{:S(2)}, u32[]{:S(2)}) collective-permute-start(bf16[384,128]{1,0:T(8,128)(2,1)S(1)} %get-tuple-element.26.own_ref), channel_id=1, source_target_pairs={{0,2},{2,0},{16,18},{18,16},{1,3},{3,1},{17,19},{19,17},{4,6},{6,4... | collective-permute-start | bytes 294920 | tf_op jit(solution)/shard_map/ppermute | solution.py:239
  25.5 35.8 %copy-start = (bf16[1280,128]{1,0:T(8,128)(2,1)}, bf16[1280,128]{1,0:T(8,128)(2,1)S(1)}, u32[]{:S(2)}) copy-start(bf16[1280,128]{1,0:T(8,128)(2,1)S(1)} %shard_map.131.refs_0_.kv0_ref) | copy-start | bytes 983044
  25.5 15.8 %collective-permute-start.3 = (bf16[1280,128]{1,0:T(8,128)(2,1)S(1)}, bf16[1280,128]{1,0:T(8,128)(2,1)S(1)}, u32[]{:S(2)}, u32[]{:S(2)}) collective-permute-start(bf16[1280,128]{1,0:T(8,128)(2,1)S(1)} %shard_map.131.refs_0_.kv0_ref), channel_id=1, source_target_pairs={{0,4},{4,8},{8,12},{12,0},{1,5},{5,9},{9,13},{13,1},{2,6},{6,10},{... | collective-permute-start | bytes 983048 | tf_op jit(solution)/shard_map/ppermute | solution.py:235
  27.0 16.1 %collective-permute-start.4 = (bf16[1280,128]{1,0:T(8,128)(2,1)S(1)}, bf16[1280,128]{1,0:T(8,128)(2,1)S(1)}, u32[]{:S(2)}, u32[]{:S(2)}) collective-permute-start(bf16[1280,128]{1,0:T(8,128)(2,1)S(1)} %shard_map.131.refs_0_.kv0_ref), channel_id=1, source_target_pairs={{0,8},{4,12},{8,0},{12,4},{1,9},{5,13},{9,1},{13,5},{2,10},{6,14},... | collective-permute-start | bytes 983048 | tf_op jit(solution)/shard_map/ppermute | solution.py:235
  29.8 13.3 %collective-permute-start.5 = (bf16[1280,128]{1,0:T(8,128)(2,1)S(1)}, bf16[1280,128]{1,0:T(8,128)(2,1)S(1)}, u32[]{:S(2)}, u32[]{:S(2)}) collective-permute-start(bf16[1280,128]{1,0:T(8,128)(2,1)S(1)} %shard_map.131.refs_0_.kv0_ref), channel_id=1, source_target_pairs={{0,12},{4,0},{8,4},{12,8},{1,13},{5,1},{9,5},{13,9},{2,14},{6,2},{... | collective-permute-start | bytes 983048 | tf_op jit(solution)/shard_map/ppermute | solution.py:235
  32.6 28.6 %all-to-all-start.1 = ((bf16[8,48,1024]{2,1,0:T(8,128)(2,1)}), bf16[8,48,1024]{2,1,0:T(8,128)(2,1)S(1)}, u32[]{:S(2)}, u32[]{:S(2)}) async-start(bf16[8,48,1024]{2,1,0:T(8,128)(2,1)} %shard_map.129), calls=%async_computation.1 | async-start | bytes 1572864 | tf_op jit(solution)/shard_map/all_to_all | solution.py:31
  41.3 27.9 %copy-start.1 = (bf16[1280,128]{1,0:T(8,128)(2,1)}, bf16[1280,128]{1,0:T(8,128)(2,1)S(1)}, u32[]{:S(2)}) copy-start(bf16[1280,128]{1,0:T(8,128)(2,1)S(1)} %collective-permute-done.3.refs_1_.kv1_ref) | copy-start | bytes 983044
  43.1 26.1 %copy-start.2 = (bf16[1280,128]{1,0:T(8,128)(2,1)}, bf16[1280,128]{1,0:T(8,128)(2,1)S(1)}, u32[]{:S(2)}) copy-start(bf16[1280,128]{1,0:T(8,128)(2,1)S(1)} %collective-permute-done.4.refs_2_.kv2_ref) | copy-start | bytes 983044
  43.1 26.1 %copy-start.3 = (bf16[1280,128]{1,0:T(8,128)(2,1)}, bf16[1280,128]{1,0:T(8,128)(2,1)S(1)}, u32[]{:S(2)}) copy-start(bf16[1280,128]{1,0:T(8,128)(2,1)S(1)} %collective-permute-done.5.refs_3_.kv3_ref) | copy-start | bytes 983044
  69.2 6.1 %copy-start.12 = (bf16[1024,128]{1,0:T(8,128)(2,1)S(1)}, bf16[1024,128]{1,0:T(8,128)(2,1)}, u32[]{:S(2)}) copy-start(bf16[1024,128]{1,0:T(8,128)(2,1)} %get-tuple-element.30) | copy-start | bytes 786436
  69.2 8.9 %copy-start.11 = (bf16[1024,128]{1,0:T(8,128)(2,1)S(1)}, bf16[1024,128]{1,0:T(8,128)(2,1)}, u32[]{:S(2)}) copy-start(bf16[1024,128]{1,0:T(8,128)(2,1)} %get-tuple-element.31) | copy-start | bytes 786436
  69.2 9.7 %copy-start.10 = (bf16[1024,128]{1,0:T(8,128)(2,1)S(1)}, bf16[1024,128]{1,0:T(8,128)(2,1)}, u32[]{:S(2)}) copy-start(bf16[1024,128]{1,0:T(8,128)(2,1)} %get-tuple-element.32) | copy-start | bytes 786436
  69.3 39.3 %all-to-all-start.2 = ((bf16[128,8,512]{2,1,0:T(8,128)(2,1)}), bf16[128,8,512]{2,1,0:T(8,128)(2,1)S(1)}, u32[]{:S(2)}, u32[]{:S(2)}) async-start(bf16[128,8,512]{2,1,0:T(8,128)(2,1)} %get-tuple-element.28), calls=%async_computation.2 | async-start | bytes 2097152 | tf_op jit(solution)/shard_map/all_to_all | solution.py:31
  75.3 22.5 %collective-permute-start.6 = (bf16[1024,128]{1,0:T(8,128)(2,1)S(1)}, bf16[1024,128]{1,0:T(8,128)(2,1)S(1)}, u32[]{:S(2)}, u32[]{:S(2)}) collective-permute-start(bf16[1024,128]{1,0:T(8,128)(2,1)S(1)} %copy-done.12), channel_id=1, source_target_pairs={{0,12},{4,0},{8,4},{12,8},{1,13},{5,1},{9,5},{13,9},{2,14},{6,2},{... | collective-permute-start | bytes 786440 | tf_op jit(solution)/shard_map/ppermute | solution.py:235
  78.1 19.7 %collective-permute-start.7 = (bf16[1024,128]{1,0:T(8,128)(2,1)S(1)}, bf16[1024,128]{1,0:T(8,128)(2,1)S(1)}, u32[]{:S(2)}, u32[]{:S(2)}) collective-permute-start(bf16[1024,128]{1,0:T(8,128)(2,1)S(1)} %copy-done.11), channel_id=1, source_target_pairs={{0,8},{4,12},{8,0},{12,4},{1,9},{5,13},{9,1},{13,5},{2,10},{6,14},... | collective-permute-start | bytes 786440 | tf_op jit(solution)/shard_map/ppermute | solution.py:235
  79.0 21.7 %copy-start.4 = (bf16[1024,128]{1,0:T(8,128)(2,1)S(1)}, bf16[1024,128]{1,0:T(8,128)(2,1)}, u32[]{:S(2)}) copy-start(bf16[1024,128]{1,0:T(8,128)(2,1)} %get-tuple-element.35.a_ref) | copy-start | bytes 786436
  79.0 21.7 %collective-permute-start.8 = (bf16[1024,128]{1,0:T(8,128)(2,1)S(1)}, bf16[1024,128]{1,0:T(8,128)(2,1)S(1)}, u32[]{:S(2)}, u32[]{:S(2)}) collective-permute-start(bf16[1024,128]{1,0:T(8,128)(2,1)S(1)} %copy-done.10), channel_id=1, source_target_pairs={{0,4},{4,8},{8,12},{12,0},{1,5},{5,9},{9,13},{13,1},{2,6},{6,10},{... | collective-permute-start | bytes 786440 | tf_op jit(solution)/shard_map/ppermute | solution.py:235
  100.8 7.8 %copy-start.5 = (f32[32,1792]{1,0:T(8,128)S(1)}, f32[32,1792]{1,0:T(8,128)}, u32[]{:S(2)}) copy-start(f32[32,1792]{1,0:T(8,128)} %get-tuple-element.34.own_ref) | copy-start | bytes 688132
  100.8 6.0 %collective-permute-start.10 = (bf16[256,128]{1,0:T(8,128)(2,1)S(1)}, bf16[256,128]{1,0:T(8,128)(2,1)S(1)}, u32[]{:S(2)}, u32[]{:S(2)}) collective-permute-start(bf16[256,128]{1,0:T(8,128)(2,1)S(1)} %get-tuple-element.41), channel_id=1, source_target_pairs={{0,16},{2,18},{16,0},{18,2},{1,17},{3,19},{17,1},{19,3},{4,20},{6,... | collective-permute-start | bytes 196616 | tf_op jit(solution)/shard_map/ppermute | solution.py:239
  103.3 4.5 %collective-permute-start.11 = (bf16[256,128]{1,0:T(8,128)(2,1)S(1)}, bf16[256,128]{1,0:T(8,128)(2,1)S(1)}, u32[]{:S(2)}, u32[]{:S(2)}) collective-permute-start(bf16[256,128]{1,0:T(8,128)(2,1)S(1)} %get-tuple-element.42), channel_id=1, source_target_pairs={{0,18},{2,16},{16,2},{18,0},{1,19},{3,17},{17,3},{19,1},{4,22},{6,... | collective-permute-start | bytes 196616 | tf_op jit(solution)/shard_map/ppermute | solution.py:239
  103.3 4.6 %collective-permute-start.9 = (bf16[256,128]{1,0:T(8,128)(2,1)S(1)}, bf16[256,128]{1,0:T(8,128)(2,1)S(1)}, u32[]{:S(2)}, u32[]{:S(2)}) collective-permute-start(bf16[256,128]{1,0:T(8,128)(2,1)S(1)} %get-tuple-element.40), channel_id=1, source_target_pairs={{0,2},{2,0},{16,18},{18,16},{1,3},{3,1},{17,19},{19,17},{4,6},{6,4... | collective-permute-start | bytes 196616 | tf_op jit(solution)/shard_map/ppermute | solution.py:239

commit v3 on v2

--- a/solution.py
+++ b/solution.py
@@ -60,26 +60,24 @@
     pick_g = jnp.where(hit & (row % 8 >= 4), 1.0, 0.0).astype(BF16)
     lane, head_of, piece = stat_lanes((64, HEAD_WIDTH))
     pick_q_low = pick_q.astype(BF16)
-    for half in range(2):
-        lanes = slice(half * STATS, (half + 1) * STATS)
-        both = dot(pick_q_low, q_ref[:, lanes], 1, 0) + dot(pick_g, g_ref[:, lanes], 1, 0)
-        out_ref[:, half, :, 0:STATS] = both.reshape(8, 8, STATS).astype(BF16)
-        product = dot(pick_q_low, o_ref[:, lanes], 1, 0) * dot(pick_q_low, g_ref[:, lanes], 1, 0)
-        stat = jnp.zeros((64, HEAD_WIDTH), F32)
-        for inner in range(GROUP):
-            mine = head_of == inner
-            part = product[:, inner * HEAD_WIDTH : (inner + 1) * HEAD_WIDTH]
-            delta = jnp.sum(part, axis=1, keepdims=True)
-            norm = norm_ref[half * GROUP + inner]
-            norm = jnp.sum(pick_q * norm, axis=1, keepdims=True) * math.sqrt(HEAD_WIDTH)
-            stat = jnp.where(mine & (lane < 3 * GROUP), norm, stat)
-            stat = jnp.where(mine & (lane >= 3 * GROUP) & (lane < 6 * GROUP), delta, stat)
-        high = stat.astype(BF16).astype(F32)
-        middle = (stat - high).astype(BF16).astype(F32)
-        low = stat - high - middle
-        stat = jnp.where(piece == 0, high, jnp.where(piece == 1, middle, low))
-        stat = jnp.where(lane == 6 * GROUP, live.astype(F32), stat)
-        out_ref[:, half, :, STATS:] = stat.reshape(8, 8, HEAD_WIDTH).astype(BF16)
+    both = dot(pick_q_low, q_ref[...], 1, 0) + dot(pick_g, g_ref[...], 1, 0)
+    out_ref[:, 0, :, 0:STATS] = both.reshape(8, 8, STATS).astype(BF16)
+    product = dot(pick_q_low, o_ref[...], 1, 0) * dot(pick_q_low, g_ref[...], 1, 0)
+    stat = jnp.zeros((64, HEAD_WIDTH), F32)
+    for inner in range(GROUP):
+        mine = head_of == inner
+        part = product[:, inner * HEAD_WIDTH : (inner + 1) * HEAD_WIDTH]
+        delta = jnp.sum(part, axis=1, keepdims=True)
+        norm = norm_ref[inner]
+        norm = jnp.sum(pick_q * norm, axis=1, keepdims=True) * math.sqrt(HEAD_WIDTH)
+        stat = jnp.where(mine & (lane < 3 * GROUP), norm, stat)
+        stat = jnp.where(mine & (lane >= 3 * GROUP) & (lane < 6 * GROUP), delta, stat)
+    high = stat.astype(BF16).astype(F32)
+    middle = (stat - high).astype(BF16).astype(F32)
+    low = stat - high - middle
+    stat = jnp.where(piece == 0, high, jnp.where(piece == 1, middle, low))
+    stat = jnp.where(lane == 6 * GROUP, live.astype(F32), stat)
+    out_ref[:, 0, :, STATS:] = stat.reshape(8, 8, HEAD_WIDTH).astype(BF16)
 
 
 def compact_kernel(p_ref, z_ref, rows_ref, out_ref):
@@ -212,12 +210,15 @@
     out_ref[1152:1280, :] = beside_ref[256:384, :]
 
 
-def x_sum_kernel(a_ref, b_ref, c_ref, d_ref, *out_refs):
+def relay_kernel(own_ref, relayed_ref, out_ref):
+    out_ref[...] = (own_ref[...].astype(F32) + relayed_ref[...].astype(F32)).astype(BF16)
+
+
+def x_sum_kernel(a_ref, b_ref, c_ref, *out_refs):
     for k, out_ref in enumerate(out_refs):
         rows = slice(256 * k, 256 * k + 256)
         total = a_ref[rows, :].astype(F32) + b_ref[rows, :].astype(F32)
-        total = total + c_ref[rows, :].astype(F32) + d_ref[rows, :].astype(F32)
-        out_ref[...] = total.astype(BF16)
+        out_ref[...] = (total + c_ref[rows, :].astype(F32)).astype(BF16)
 
 
 def y_sum_kernel(info, a_ref, b_ref, c_ref, d_ref, k_ref, v_ref):
@@ -331,7 +332,11 @@
         o,
         g,
         norms,
-        in_specs=[smem] * 3 + [vmem] * 4,
+        grid=(2,),
+        in_specs=[smem] * 3
+        + [pl.BlockSpec((slice_rows, STATS), lambda k: (0, k))] * 3
+        + [pl.BlockSpec((GROUP, 1, slice_rows), lambda k: (k, 0, 0))],
+        out_specs=pl.BlockSpec((8, 1, 8, 1024), lambda k: (0, k, 0, 0)),
         small=False,
     )
     arrived = exchange(picked.reshape(16, 8, 1024), SAMPLE)
@@ -381,6 +386,12 @@
     out_slot = slot_of.reshape(16, spans, 1, 4) + LIVE * jnp.arange(2)[None, None, :, None]
     out_slot = out_slot.reshape(1, 1024)
 
+    kv_grads, gq_parts = prompt_terms(in_slot, out_slot, rows, *kv)
+    relayed = shifted(kv_grads[2], -1)
+    ahead = shifted(kv_grads[3], 1)
+    gq_parts = exchange(gq_parts, SAMPLE_SPAN)
+    joined = call(relay_kernel, packed(1024), kv_grads[1], relayed)
+    behind = shifted(joined, -1)
     own_rows = slice_rows // spans
     own_shape = jax.ShapeDtypeStruct((own_rows, 2 * HEAD_WIDTH), BF16)
     gk_self, gv_self, gq_self = call(
@@ -396,12 +407,7 @@
         in_specs=[smem] * 2 + [vmem] * 8,
         small=False,
     )
-
-    kv_grads, gq_parts = prompt_terms(in_slot, out_slot, rows, *kv)
-    parts = [kv_grads[0]] + [shifted(kv_grads[k], -k) for k in (1, 2, 3)]
-    gq_parts = exchange(gq_parts, SAMPLE_SPAN)
-    *parts, gq_self = lax.optimization_barrier((*parts, gq_self))
-    parts = call(x_sum_kernel, [packed(256)] * 4, *parts)
+    parts = call(x_sum_kernel, [packed(256)] * 4, kv_grads[0], ahead, behind)
     parts = [parts[0]] + [crossed(parts[k], k) for k in (1, 2, 3)]
     prompt_shape = jax.ShapeDtypeStruct(prompt_key_rows.shape, BF16)
     gk_prompt, gv_prompt = call(

time: 111 us -> 118 us (1.063)
  waiting for transfers between devices: 39.1 us -> 43.7 us
  starting transfers between devices: 42.9 us -> 45.1 us
    ppermute x6, waiting for transfers between devices: 13.2 us -> 20.1 us  [shifted(): return lax.ppermute(value, ALONG_X, [(k, (k + by) % 4) for k in range(4)])]
    ppermute x6, waiting for transfers between devices: 7.74 us -> 5.46 us  [crossed(): return lax.ppermute(value, ALONG_Y, [(k, k ^ by) for k in range(4)])]
    ppermute x6, starting transfers between devices: 10.2 us -> 12.3 us  [shifted(): return lax.ppermute(value, ALONG_X, [(k, (k + by) % 4) for k in range(4)])]
    pallas_call x9 -> x10, Pallas kernels: 23.7 us -> 23.5 us  [call(): pl.pallas_call(body, out_shape=out_shape, interpret=INTERPRET, compiler_p...]
  transfers between devices with their start and end apart: 15 -> 15, of which waited for: 10 -> 7; matrix products, arithmetic and copies ran while one was open for 2% -> 2% of each run, Pallas kernels for 11% -> 10%
where the time goes in v3:
time: 118 us; the launch traced here: 116 us
  starting transfers between devices  45.1 us (38%)
  waiting for transfers between devices  43.7 us (37%)
  Pallas kernels  23.5 us (20%)
  other arithmetic  1.6 us (1%)
  between operations  1.54 us (1%)
    pallas_call x10, Pallas kernels, call(): pl.pallas_call(body, out_shape=out_shape, interpret=INTERPRET, compiler_p...  23.5 us
    all_to_all x3, starting transfers between devices, exchange(): return lax.all_to_all(tiles, axes, split_axis=0, concat_axis=0, tiled=True)  23.2 us
    ppermute x6, waiting for transfers between devices, shifted(): return lax.ppermute(value, ALONG_X, [(k, (k + by) % 4) for k in range(4)])  20.1 us
    all_to_all x3, waiting for transfers between devices, exchange(): return lax.all_to_all(tiles, axes, split_axis=0, concat_axis=0, tiled=True)  18.2 us
    ppermute x6, starting transfers between devices, shifted(): return lax.ppermute(value, ALONG_X, [(k, (k + by) % 4) for k in range(4)])  12.3 us
    ppermute x6, starting transfers between devices, crossed(): return lax.ppermute(value, ALONG_Y, [(k, k ^ by) for k in range(4)])  9.65 us
    ppermute x6, waiting for transfers between devices, crossed(): return lax.ppermute(value, ALONG_Y, [(k, k ^ by) for k in range(4)])  5.46 us
  transfers between devices with their start and end apart: 15, of which 7 were waited for; matrix products, arithmetic and copies ran while one was open for 2% of the time, Pallas kernels for 10%

profile of v3, /device:TPU:8, one launch (start us, length us, event | category | flops | bytes accessed | tf_op | source)
XLA Modules:
  0.0 116.3 jit_solution(12984901786672786285)
XLA Ops:
  1.3 3.0 %shard_map.128 = bf16[8,2,8,1024]{3,2,1,0:T(8,128)(2,1)} custom-call(s32[1]{0:T(128)} %bitcast.p_ref, s32[1]{0:T(128)} %bitcast.1.turn_ref, s32[1]{0:T(128)S(6)} %copy.17.live_ref, bf16[256,1792]{1,0:T(8,128)(2,1)} %bitcast.17, bf16[256,1792]{1,0:T(8,128)(2,1)} %bitcast.19, bf16[256,1792]{1,0:T(8,128)(2,1)} %bitcast.21, f32[14,1,256]{2,1,0:T(1,128)} %bitcast.26), custom_call_target="tpu_custom_call" | custom-call | tf_op jit(solution)/shard_map/pallas_call | solution.py:40
  4.3 0.0 copy-start.10
  4.3 10.4 %all-to-all-start = ((bf16[16,8,1024]{2,1,0:T(8,128)(2,1)}), bf16[16,8,1024]{2,1,0:T(8,128)(2,1)S(1)}, u32[]{:S(2)}, u32[]{:S(2)}) async-start(bf16[16,8,1024]{2,1,0:T(8,128)(2,1)} %bitcast.23), calls=%async_computation | async-start | bytes 524288 | tf_op jit(solution)/shard_map/all_to_all | solution.py:31
  14.9 3.5 %collective-permute-start.1 = (bf16[256,128]{1,0:T(8,128)(2,1)S(1)}, bf16[256,128]{1,0:T(8,128)(2,1)S(1)}, u32[]{:S(2)}, u32[]{:S(2)}) collective-permute-start(bf16[256,128]{1,0:T(8,128)(2,1)S(1)} %get-tuple-element.22), channel_id=1, source_target_pairs={{0,16},{2,18},{16,0},{18,2},{1,17},{3,19},{17,1},{19,3},{4,20},{6,... | collective-permute-start | bytes 196616 | tf_op jit(solution)/shard_map/ppermute | solution.py:240
  18.4 0.0 collective-permute-start.2
  18.4 1.3 %collective-permute-start = (bf16[384,128]{1,0:T(8,128)(2,1)S(1)}, bf16[384,128]{1,0:T(8,128)(2,1)S(1)}, u32[]{:S(2)}, u32[]{:S(2)}) collective-permute-start(bf16[384,128]{1,0:T(8,128)(2,1)S(1)} %get-tuple-element.21.own_ref), channel_id=1, source_target_pairs={{0,2},{2,0},{16,18},{18,16},{1,3},{3,1},{17,19},{19,17},{4,6},{6,4... | collective-permute-start | bytes 294920 | tf_op jit(solution)/shard_map/ppermute | solution.py:240
  19.8 1.5 %collective-permute-done.1.third_ref = bf16[256,128]{1,0:T(8,128)(2,1)S(1)} collective-permute-done((bf16[256,128]{1,0:T(8,128)(2,1)S(1)}, bf16[256,128]{1,0:T(8,128)(2,1)S(1)}, u32[]{:S(2)}, u32[]{:S(2)}) %collective-permute-start.1) | collective-permute-done | bytes 65568 | tf_op jit(solution)/shard_map/ppermute | solution.py:240
  21.3 2.0 %collective-permute-done.2.fourth_ref = bf16[256,128]{1,0:T(8,128)(2,1)S(1)} collective-permute-done((bf16[256,128]{1,0:T(8,128)(2,1)S(1)}, bf16[256,128]{1,0:T(8,128)(2,1)S(1)}, u32[]{:S(2)}, u32[]{:S(2)}) %collective-permute-start.2) | collective-permute-done | bytes 65568 | tf_op jit(solution)/shard_map/ppermute | solution.py:240
  23.3 1.9 %collective-permute-done.beside_ref = bf16[384,128]{1,0:T(8,128)(2,1)S(1)} collective-permute-done((bf16[384,128]{1,0:T(8,128)(2,1)S(1)}, bf16[384,128]{1,0:T(8,128)(2,1)S(1)}, u32[]{:S(2)}, u32[]{:S(2)}) %collective-permute-start) | collective-permute-done | bytes 98336 | tf_op jit(solution)/shard_map/ppermute | solution.py:240
  25.2 1.6 %collective-permute-start.3 = (bf16[1280,128]{1,0:T(8,128)(2,1)S(1)}, bf16[1280,128]{1,0:T(8,128)(2,1)S(1)}, u32[]{:S(2)}, u32[]{:S(2)}) collective-permute-start(bf16[1280,128]{1,0:T(8,128)(2,1)S(1)} %shard_map.131.refs_0_.kv0_ref), channel_id=1, source_target_pairs={{0,4},{4,8},{8,12},{12,0},{1,5},{5,9},{9,13},{13,1},{2,6},{6,10},{... | collective-permute-start | bytes 983048 | tf_op jit(solution)/shard_map/ppermute | solution.py:236
  26.8 2.7 %collective-permute-start.4 = (bf16[1280,128]{1,0:T(8,128)(2,1)S(1)}, bf16[1280,128]{1,0:T(8,128)(2,1)S(1)}, u32[]{:S(2)}, u32[]{:S(2)}) collective-permute-start(bf16[1280,128]{1,0:T(8,128)(2,1)S(1)} %shard_map.131.refs_0_.kv0_ref), channel_id=1, source_target_pairs={{0,8},{4,12},{8,0},{12,4},{1,9},{5,13},{9,1},{13,5},{2,10},{6,14},... | collective-permute-start | bytes 983048 | tf_op jit(solution)/shard_map/ppermute | solution.py:236
  29.5 1.4 %collective-permute-start.5 = (bf16[1280,128]{1,0:T(8,128)(2,1)S(1)}, bf16[1280,128]{1,0:T(8,128)(2,1)S(1)}, u32[]{:S(2)}, u32[]{:S(2)}) collective-permute-start(bf16[1280,128]{1,0:T(8,128)(2,1)S(1)} %shard_map.131.refs_0_.kv0_ref), channel_id=1, source_target_pairs={{0,12},{4,0},{8,4},{12,8},{1,13},{5,1},{9,5},{13,9},{2,14},{6,2},{... | collective-permute-start | bytes 983048 | tf_op jit(solution)/shard_map/ppermute | solution.py:236
  31.0 0.0 all-to-all-done.rows_ref
  31.0 1.4 %shard_map.129 = bf16[8,48,1024]{2,1,0:T(8,128)(2,1)} custom-call(s32[1]{0:T(128)} %bitcast.p_ref, s32[1]{0:T(128)} %bitcast.8.z_ref, bf16[16,8,1024]{2,1,0:T(8,128)(2,1)S(1)} %all-to-all-done.rows_ref), custom_call_target="tpu_custom_call" | custom-call | tf_op jit(solution)/shard_map/pallas_call | solution.py:40
  32.4 6.5 %all-to-all-start.1 = ((bf16[8,48,1024]{2,1,0:T(8,128)(2,1)}), bf16[8,48,1024]{2,1,0:T(8,128)(2,1)S(1)}, u32[]{:S(2)}, u32[]{:S(2)}) async-start(bf16[8,48,1024]{2,1,0:T(8,128)(2,1)} %shard_map.129), calls=%async_computation.1 | async-start | bytes 1572864 | tf_op jit(solution)/shard_map/all_to_all | solution.py:31
  38.9 0.4 fusion.5
  39.4 0.1 fusion.11
  39.5 0.1 select_reduce_fusion.2
  39.6 0.4 select_reduce_fusion.1
  40.0 0.1 select_reduce_fusion
  40.1 0.1 copy.15
  40.2 0.1 add_select_fusion
  40.3 0.1 copy.16
  40.4 0.1 iota_add_fusion
  40.5 0.1 broadcast_add_fusion
  40.6 0.1 iota_compare_fusion.3
  40.7 0.2 add.190.out_slot_ref
  40.9 0.1 add_select_fusion.2
  40.9 0.1 select_n.95.in_slot_ref
  41.0 0.0 collective-permute-done.3.refs_1_.kv1_ref
  41.1 1.8 %collective-permute-done.4.refs_2_.kv2_ref = bf16[1280,128]{1,0:T(8,128)(2,1)S(1)} collective-permute-done((bf16[1280,128]{1,0:T(8,128)(2,1)S(1)}, bf16[1280,128]{1,0:T(8,128)(2,1)S(1)}, u32[]{:S(2)}, u32[]{:S(2)}) %collective-permute-start.4) | collective-permute-done | bytes 327712 | tf_op jit(solution)/shard_map/ppermute | solution.py:236
  42.9 0.0 collective-permute-done.5.refs_3_.kv3_ref
  42.9 18.2 %all-to-all-done.1.rows_ref = bf16[8,48,1024]{2,1,0:T(8,128)(2,1)S(1)} async-done(((bf16[8,48,1024]{2,1,0:T(8,128)(2,1)}), bf16[8,48,1024]{2,1,0:T(8,128)(2,1)S(1)}, u32[]{:S(2)}, u32[]{:S(2)}) %all-to-all-start.1) | async-done | bytes 786464 | tf_op jit(solution)/shard_map/all_to_all | solution.py:31
  61.0 8.0 %shard_map.132 = (bf16[1024,128]{1,0:T(8,128)(2,1)}, bf16[1024,128]{1,0:T(8,128)(2,1)}, bf16[1024,128]{1,0:T(8,128)(2,1)}, bf16[1024,128]{1,0:T(8,128)(2,1)}, bf16[128,8,512]{2,1,0:T(8,128)(2,1)}) custom-call(s32[1,384]{1,0:T(1,128)S(1)} %select_n.95.in_slot_ref, s32[1,1024]{1,0:T(1,128)S(1)} %add.190.out_slot_ref, ...), custom_call_target="tpu_custom_call" | custom-call | tf_op jit(solution)/shard_map/pallas_call | solution.py:40
  69.0 6.3 %all-to-all-start.2 = ((bf16[128,8,512]{2,1,0:T(8,128)(2,1)}), bf16[128,8,512]{2,1,0:T(8,128)(2,1)S(1)}, u32[]{:S(2)}, u32[]{:S(2)}) async-start(bf16[128,8,512]{2,1,0:T(8,128)(2,1)} %get-tuple-element.23), calls=%async_computation.2 | async-start | bytes 2097152 | tf_op jit(solution)/shard_map/all_to_all | solution.py:31
  75.3 2.8 %collective-permute-start.7 = (bf16[1024,128]{1,0:T(8,128)(2,1)S(1)}, bf16[1024,128]{1,0:T(8,128)(2,1)S(1)}, u32[]{:S(2)}, u32[]{:S(2)}) collective-permute-start(bf16[1024,128]{1,0:T(8,128)(2,1)S(1)} %copy-done.12), channel_id=1, source_target_pairs={{0,12},{4,0},{8,4},{12,8},{1,13},{5,1},{9,5},{13,9},{2,14},{6,2},{... | collective-permute-start | bytes 786440 | tf_op jit(solution)/shard_map/ppermute | solution.py:236
  78.1 9.8 %collective-permute-done.7.relayed_ref = bf16[1024,128]{1,0:T(8,128)(2,1)S(1)} collective-permute-done((bf16[1024,128]{1,0:T(8,128)(2,1)S(1)}, bf16[1024,128]{1,0:T(8,128)(2,1)S(1)}, u32[]{:S(2)}, u32[]{:S(2)}) %collective-permute-start.7) | collective-permute-done | bytes 262176 | tf_op jit(solution)/shard_map/ppermute | solution.py:236
  88.0 0.1 shard_map.135
  88.0 3.7 %collective-permute-start.8 = (bf16[1024,128]{1,0:T(8,128)(2,1)S(1)}, bf16[1024,128]{1,0:T(8,128)(2,1)S(1)}, u32[]{:S(2)}, u32[]{:S(2)}) collective-permute-start(bf16[1024,128]{1,0:T(8,128)(2,1)S(1)} %shard_map.135), channel_id=1, source_target_pairs={{0,12},{4,0},{8,4},{12,8},{1,13},{5,1},{9,5},{13,9},{2,14},{6,2},{... | collective-permute-start | bytes 786440 | tf_op jit(solution)/shard_map/ppermute | solution.py:236
  91.8 8.4 %collective-permute-done.8.c_ref = bf16[1024,128]{1,0:T(8,128)(2,1)S(1)} collective-permute-done((bf16[1024,128]{1,0:T(8,128)(2,1)S(1)}, bf16[1024,128]{1,0:T(8,128)(2,1)S(1)}, u32[]{:S(2)}, u32[]{:S(2)}) %collective-permute-start.8) | collective-permute-done | bytes 262176 | tf_op jit(solution)/shard_map/ppermute | solution.py:236
  100.2 0.1 shard_map.136
  100.3 0.6 collective-permute-start.10
  100.9 1.7 %collective-permute-start.11 = (bf16[256,128]{1,0:T(8,128)(2,1)S(1)}, bf16[256,128]{1,0:T(8,128)(2,1)S(1)}, u32[]{:S(2)}, u32[]{:S(2)}) collective-permute-start(bf16[256,128]{1,0:T(8,128)(2,1)S(1)} %get-tuple-element.32), channel_id=1, source_target_pairs={{0,18},{2,16},{16,2},{18,0},{1,19},{3,17},{17,3},{19,1},{4,22},{6,... | collective-permute-start | bytes 196616 | tf_op jit(solution)/shard_map/ppermute | solution.py:240
  102.6 2.5 %collective-permute-start.9 = (bf16[256,128]{1,0:T(8,128)(2,1)S(1)}, bf16[256,128]{1,0:T(8,128)(2,1)S(1)}, u32[]{:S(2)}, u32[]{:S(2)}) collective-permute-start(bf16[256,128]{1,0:T(8,128)(2,1)S(1)} %get-tuple-element.30), channel_id=1, source_target_pairs={{0,2},{2,0},{16,18},{18,16},{1,3},{3,1},{17,19},{19,17},{4,6},{6,4... | collective-permute-start | bytes 196616 | tf_op jit(solution)/shard_map/ppermute | solution.py:240
  105.1 9.4 %shard_map.133 = (bf16[32,256]{1,0:T(8,128)(2,1)}, bf16[32,256]{1,0:T(8,128)(2,1)}, f32[32,1792]{1,0:T(8,128)}) custom-call(s32[1]{0:T(128)} %bitcast.p_ref, s32[1]{0:T(128)S(6)} %copy.17.live_ref, bf16[256,1792]{1,0:T(8,128)(2,1)} %bitcast.18, bf16[256,1792]{1,0:T(8,128)(2,1)} %bitcast.20, bf16[256,1792]{1,0:T(8,128)(2,1)} %bitcast.22, ...), custom_call_target="tpu_custom_call" | custom-call | tf_op jit(solution)/shard_map/pallas_call | solution.py:40
  114.5 0.7 shard_map.137
  115.2 0.3 copy-done.6
  115.5 0.8 shard_map.134
  (38 shorter events, 0.2 us)
Async XLA Ops:
  4.3 10.5 %copy-start.7 = (bf16[128,256]{1,0:T(8,128)(2,1)S(1)}, bf16[128,256]{1,0:T(8,128)(2,1)}, u32[]{:S(2)}) copy-start(bf16[128,256]{1,0:T(8,128)(2,1)} %pk_ref.1) | copy-start | bytes 196612
  4.3 10.5 %copy-start.8 = (bf16[128,256]{1,0:T(8,128)(2,1)S(1)}, bf16[128,256]{1,0:T(8,128)(2,1)}, u32[]{:S(2)}) copy-start(bf16[128,256]{1,0:T(8,128)(2,1)} %pv_ref.1) | copy-start | bytes 196612
  4.3 10.5 %copy-start.9 = (bf16[1,32,256]{2,1,0:T(8,128)(2,1)S(1)}, bf16[1,32,256]{2,1,0:T(8,128)(2,1)}, u32[]{:S(2)}) copy-start(bf16[1,32,256]{2,1,0:T(8,128)(2,1)} %param.16) | copy-start | bytes 49156
  4.3 10.5 %copy-start.10 = (bf16[1,32,256]{2,1,0:T(8,128)(2,1)S(1)}, bf16[1,32,256]{2,1,0:T(8,128)(2,1)}, u32[]{:S(2)}) copy-start(bf16[1,32,256]{2,1,0:T(8,128)(2,1)} %param.17) | copy-start | bytes 49156
  4.3 26.7 %all-to-all-start = ((bf16[16,8,1024]{2,1,0:T(8,128)(2,1)}), bf16[16,8,1024]{2,1,0:T(8,128)(2,1)S(1)}, u32[]{:S(2)}, u32[]{:S(2)}) async-start(bf16[16,8,1024]{2,1,0:T(8,128)(2,1)} %bitcast.23), calls=%async_computation | async-start | bytes 524288 | tf_op jit(solution)/shard_map/all_to_all | solution.py:31
  14.9 6.4 %collective-permute-start.1 = (bf16[256,128]{1,0:T(8,128)(2,1)S(1)}, bf16[256,128]{1,0:T(8,128)(2,1)S(1)}, u32[]{:S(2)}, u32[]{:S(2)}) collective-permute-start(bf16[256,128]{1,0:T(8,128)(2,1)S(1)} %get-tuple-element.22), channel_id=1, source_target_pairs={{0,16},{2,18},{16,0},{18,2},{1,17},{3,19},{17,1},{19,3},{4,20},{6,... | collective-permute-start | bytes 196616 | tf_op jit(solution)/shard_map/ppermute | solution.py:240
  18.4 5.0 %collective-permute-start.2 = (bf16[256,128]{1,0:T(8,128)(2,1)S(1)}, bf16[256,128]{1,0:T(8,128)(2,1)S(1)}, u32[]{:S(2)}, u32[]{:S(2)}) collective-permute-start(bf16[256,128]{1,0:T(8,128)(2,1)S(1)} %get-tuple-element.22), channel_id=1, source_target_pairs={{0,18},{2,16},{16,2},{18,0},{1,19},{3,17},{17,3},{19,1},{4,22},{6,... | collective-permute-start | bytes 196616 | tf_op jit(solution)/shard_map/ppermute | solution.py:240
  18.4 6.8 %collective-permute-start = (bf16[384,128]{1,0:T(8,128)(2,1)S(1)}, bf16[384,128]{1,0:T(8,128)(2,1)S(1)}, u32[]{:S(2)}, u32[]{:S(2)}) collective-permute-start(bf16[384,128]{1,0:T(8,128)(2,1)S(1)} %get-tuple-element.21.own_ref), channel_id=1, source_target_pairs={{0,2},{2,0},{16,18},{18,16},{1,3},{3,1},{17,19},{19,17},{4,6},{6,4... | collective-permute-start | bytes 294920 | tf_op jit(solution)/shard_map/ppermute | solution.py:240
  25.2 35.8 %copy-start = (bf16[1280,128]{1,0:T(8,128)(2,1)}, bf16[1280,128]{1,0:T(8,128)(2,1)S(1)}, u32[]{:S(2)}) copy-start(bf16[1280,128]{1,0:T(8,128)(2,1)S(1)} %shard_map.131.refs_0_.kv0_ref) | copy-start | bytes 983044
  25.2 15.8 %collective-permute-start.3 = (bf16[1280,128]{1,0:T(8,128)(2,1)S(1)}, bf16[1280,128]{1,0:T(8,128)(2,1)S(1)}, u32[]{:S(2)}, u32[]{:S(2)}) collective-permute-start(bf16[1280,128]{1,0:T(8,128)(2,1)S(1)} %shard_map.131.refs_0_.kv0_ref), channel_id=1, source_target_pairs={{0,4},{4,8},{8,12},{12,0},{1,5},{5,9},{9,13},{13,1},{2,6},{6,10},{... | collective-permute-start | bytes 983048 | tf_op jit(solution)/shard_map/ppermute | solution.py:236
  26.8 16.1 %collective-permute-start.4 = (bf16[1280,128]{1,0:T(8,128)(2,1)S(1)}, bf16[1280,128]{1,0:T(8,128)(2,1)S(1)}, u32[]{:S(2)}, u32[]{:S(2)}) collective-permute-start(bf16[1280,128]{1,0:T(8,128)(2,1)S(1)} %shard_map.131.refs_0_.kv0_ref), channel_id=1, source_target_pairs={{0,8},{4,12},{8,0},{12,4},{1,9},{5,13},{9,1},{13,5},{2,10},{6,14},... | collective-permute-start | bytes 983048 | tf_op jit(solution)/shard_map/ppermute | solution.py:236
  29.5 13.3 %collective-permute-start.5 = (bf16[1280,128]{1,0:T(8,128)(2,1)S(1)}, bf16[1280,128]{1,0:T(8,128)(2,1)S(1)}, u32[]{:S(2)}, u32[]{:S(2)}) collective-permute-start(bf16[1280,128]{1,0:T(8,128)(2,1)S(1)} %shard_map.131.refs_0_.kv0_ref), channel_id=1, source_target_pairs={{0,12},{4,0},{8,4},{12,8},{1,13},{5,1},{9,5},{13,9},{2,14},{6,2},{... | collective-permute-start | bytes 983048 | tf_op jit(solution)/shard_map/ppermute | solution.py:236
  32.4 28.6 %all-to-all-start.1 = ((bf16[8,48,1024]{2,1,0:T(8,128)(2,1)}), bf16[8,48,1024]{2,1,0:T(8,128)(2,1)S(1)}, u32[]{:S(2)}, u32[]{:S(2)}) async-start(bf16[8,48,1024]{2,1,0:T(8,128)(2,1)} %shard_map.129), calls=%async_computation.1 | async-start | bytes 1572864 | tf_op jit(solution)/shard_map/all_to_all | solution.py:31
  41.1 28.0 %copy-start.1 = (bf16[1280,128]{1,0:T(8,128)(2,1)}, bf16[1280,128]{1,0:T(8,128)(2,1)S(1)}, u32[]{:S(2)}) copy-start(bf16[1280,128]{1,0:T(8,128)(2,1)S(1)} %collective-permute-done.3.refs_1_.kv1_ref) | copy-start | bytes 983044
  42.9 26.1 %copy-start.2 = (bf16[1280,128]{1,0:T(8,128)(2,1)}, bf16[1280,128]{1,0:T(8,128)(2,1)S(1)}, u32[]{:S(2)}) copy-start(bf16[1280,128]{1,0:T(8,128)(2,1)S(1)} %collective-permute-done.4.refs_2_.kv2_ref) | copy-start | bytes 983044
  42.9 26.1 %copy-start.3 = (bf16[1280,128]{1,0:T(8,128)(2,1)}, bf16[1280,128]{1,0:T(8,128)(2,1)S(1)}, u32[]{:S(2)}) copy-start(bf16[1280,128]{1,0:T(8,128)(2,1)S(1)} %collective-permute-done.5.refs_3_.kv3_ref) | copy-start | bytes 983044
  69.0 6.3 %copy-start.12 = (bf16[1024,128]{1,0:T(8,128)(2,1)S(1)}, bf16[1024,128]{1,0:T(8,128)(2,1)}, u32[]{:S(2)}) copy-start(bf16[1024,128]{1,0:T(8,128)(2,1)} %get-tuple-element.28) | copy-start | bytes 786436
  69.0 9.1 %copy-start.11 = (bf16[1024,128]{1,0:T(8,128)(2,1)S(1)}, bf16[1024,128]{1,0:T(8,128)(2,1)}, u32[]{:S(2)}) copy-start(bf16[1024,128]{1,0:T(8,128)(2,1)} %get-tuple-element.26) | copy-start | bytes 786436
  69.0 18.9 %copy-start.5 = (bf16[1024,128]{1,0:T(8,128)(2,1)S(1)}, bf16[1024,128]{1,0:T(8,128)(2,1)}, u32[]{:S(2)}) copy-start(bf16[1024,128]{1,0:T(8,128)(2,1)} %get-tuple-element.27.own_ref) | copy-start | bytes 786436
  69.0 46.1 %all-to-all-start.2 = ((bf16[128,8,512]{2,1,0:T(8,128)(2,1)}), bf16[128,8,512]{2,1,0:T(8,128)(2,1)S(1)}, u32[]{:S(2)}, u32[]{:S(2)}) async-start(bf16[128,8,512]{2,1,0:T(8,128)(2,1)} %get-tuple-element.23), calls=%async_computation.2 | async-start | bytes 2097152 | tf_op jit(solution)/shard_map/all_to_all | solution.py:31
  75.3 12.6 %collective-permute-start.7 = (bf16[1024,128]{1,0:T(8,128)(2,1)S(1)}, bf16[1024,128]{1,0:T(8,128)(2,1)S(1)}, u32[]{:S(2)}, u32[]{:S(2)}) collective-permute-start(bf16[1024,128]{1,0:T(8,128)(2,1)S(1)} %copy-done.12), channel_id=1, source_target_pairs={{0,12},{4,0},{8,4},{12,8},{1,13},{5,1},{9,5},{13,9},{2,14},{6,2},{... | collective-permute-start | bytes 786440 | tf_op jit(solution)/shard_map/ppermute | solution.py:236
  78.1 13.6 %collective-permute-start.6 = (bf16[1024,128]{1,0:T(8,128)(2,1)S(1)}, bf16[1024,128]{1,0:T(8,128)(2,1)S(1)}, u32[]{:S(2)}, u32[]{:S(2)}) collective-permute-start(bf16[1024,128]{1,0:T(8,128)(2,1)S(1)} %copy-done.11), channel_id=1, source_target_pairs={{0,4},{4,8},{8,12},{12,0},{1,5},{5,9},{9,13},{13,1},{2,6},{6,10},{... | collective-permute-start | bytes 786440 | tf_op jit(solution)/shard_map/ppermute | solution.py:236
  88.0 12.2 %copy-start.4 = (bf16[1024,128]{1,0:T(8,128)(2,1)S(1)}, bf16[1024,128]{1,0:T(8,128)(2,1)}, u32[]{:S(2)}) copy-start(bf16[1024,128]{1,0:T(8,128)(2,1)} %get-tuple-element.25.a_ref) | copy-start | bytes 786436
  88.0 12.2 %collective-permute-start.8 = (bf16[1024,128]{1,0:T(8,128)(2,1)S(1)}, bf16[1024,128]{1,0:T(8,128)(2,1)S(1)}, u32[]{:S(2)}, u32[]{:S(2)}) collective-permute-start(bf16[1024,128]{1,0:T(8,128)(2,1)S(1)} %shard_map.135), channel_id=1, source_target_pairs={{0,12},{4,0},{8,4},{12,8},{1,13},{5,1},{9,5},{13,9},{2,14},{6,2},{... | collective-permute-start | bytes 786440 | tf_op jit(solution)/shard_map/ppermute | solution.py:236
  100.3 14.2 %collective-permute-start.10 = (bf16[256,128]{1,0:T(8,128)(2,1)S(1)}, bf16[256,128]{1,0:T(8,128)(2,1)S(1)}, u32[]{:S(2)}, u32[]{:S(2)}) collective-permute-start(bf16[256,128]{1,0:T(8,128)(2,1)S(1)} %get-tuple-element.31), channel_id=1, source_target_pairs={{0,16},{2,18},{16,0},{18,2},{1,17},{3,19},{17,1},{19,3},{4,20},{6,... | collective-permute-start | bytes 196616 | tf_op jit(solution)/shard_map/ppermute | solution.py:240
  100.9 13.6 %collective-permute-start.11 = (bf16[256,128]{1,0:T(8,128)(2,1)S(1)}, bf16[256,128]{1,0:T(8,128)(2,1)S(1)}, u32[]{:S(2)}, u32[]{:S(2)}) collective-permute-start(bf16[256,128]{1,0:T(8,128)(2,1)S(1)} %get-tuple-element.32), channel_id=1, source_target_pairs={{0,18},{2,16},{16,2},{18,0},{1,19},{3,17},{17,3},{19,1},{4,22},{6,... | collective-permute-start | bytes 196616 | tf_op jit(solution)/shard_map/ppermute | solution.py:240
  102.6 11.9 %collective-permute-start.9 = (bf16[256,128]{1,0:T(8,128)(2,1)S(1)}, bf16[256,128]{1,0:T(8,128)(2,1)S(1)}, u32[]{:S(2)}, u32[]{:S(2)}) collective-permute-start(bf16[256,128]{1,0:T(8,128)(2,1)S(1)} %get-tuple-element.30), channel_id=1, source_target_pairs={{0,2},{2,0},{16,18},{18,16},{1,3},{3,1},{17,19},{19,17},{4,6},{6,4... | collective-permute-start | bytes 196616 | tf_op jit(solution)/shard_map/ppermute | solution.py:240
  114.5 1.0 copy-start.6

commit v4 on v3

--- a/solution.py
+++ b/solution.py
@@ -259,44 +259,42 @@
     block = lane // 32
     from_span = (p // 2 + 4 - block // 2) % 4 * 2 + (p % 2 + block % 2) % 2
     position = from_span * 32 + lane % 32
-    for kv in range(2):
-        key_lanes = slice(kv * HEAD_WIDTH, (kv + 1) * HEAD_WIDTH)
-
-        def piece(ref, which, kind):
-            first = 1024 + 128 * which + 32 * (2 * kind + kv)
-            return ref[first : first + 32, :]
-
-        keys, values = piece(kv0_ref, 0, 0), piece(kv0_ref, 0, 1)
-        all_keys = jnp.concatenate([piece(r, w, 0) for r in kv_refs for w in range(2)], axis=0)
-        all_values = jnp.concatenate([piece(r, w, 1) for r in kv_refs for w in range(2)], axis=0)
-        gk = jnp.zeros((32, HEAD_WIDTH), F32)
-        gv = jnp.zeros((32, HEAD_WIDTH), F32)
-        for inner in range(GROUP):
-            head = kv * GROUP + inner
-            lanes = slice(head * HEAD_WIDTH, (head + 1) * HEAD_WIDTH)
-            q = q_ref[:, lanes]
-            g = jnp.where(live_row, g_ref[:, lanes], zero)
-            product = g.astype(F32) * o_ref[:, lanes].astype(F32)
-            delta = lax.dot_general(
-                ones, product, (((1,), (1,)), ((), ())), precision=EXACT, preferred_element_type=F32
-            )
-            prob = jnp.exp(dot(keys, q, 1, 1) * SCALE - norm_ref[head])
-            prob = jnp.where(j_row <= i_row, prob, 0.0)
-            sgrad = prob * (dot(values, g, 1, 1) - delta[0:1, :])
-            gv = gv + dot(prob.astype(BF16), g, 1, 0)
-            gk = gk + dot(sgrad.astype(BF16), q, 1, 0)
-            q_own, g_own = q_ref[own, lanes], g_ref[own, lanes]
-            g_own = jnp.where(live_own, g_own, zero)
-            product = g_own.astype(F32) * o_ref[own, lanes].astype(F32)
-            delta_own = jnp.sum(product, axis=1, keepdims=True)
-            norm_own = jnp.sum(jnp.where(diagonal, norm_ref[head], 0.0), axis=1, keepdims=True)
-            prob = jnp.exp(dot(q_own, all_keys, 1, 1) * SCALE - norm_own)
-            i_own = lax.broadcasted_iota(jnp.int32, prob.shape, 0) + p * 32
-            prob = jnp.where(position <= i_own, prob, 0.0)
-            sgrad = prob * (dot(g_own, all_values, 1, 1) - delta_own)
-            gq_ref[:, lanes] = dot(sgrad.astype(BF16), all_keys, 1, 0) * SCALE
-        gk_ref[:, key_lanes] = (gk * SCALE).astype(BF16)
-        gv_ref[:, key_lanes] = gv.astype(BF16)
+    kv = pl.program_id(0)
+    def piece(ref, which, kind):
+        first = 1024 + 128 * which + 32 * (2 * kind + kv)
+        return ref[pl.ds(pl.multiple_of(first, 32), 32), :]
+
+    keys, values = piece(kv0_ref, 0, 0), piece(kv0_ref, 0, 1)
+    all_keys = jnp.concatenate([piece(r, w, 0) for r in kv_refs for w in range(2)], axis=0)
+    all_values = jnp.concatenate([piece(r, w, 1) for r in kv_refs for w in range(2)], axis=0)
+    gk = jnp.zeros((32, HEAD_WIDTH), F32)
+    gv = jnp.zeros((32, HEAD_WIDTH), F32)
+    for inner in range(GROUP):
+        head = inner
+        lanes = slice(head * HEAD_WIDTH, (head + 1) * HEAD_WIDTH)
+        q = q_ref[:, lanes]
+        g = jnp.where(live_row, g_ref[:, lanes], zero)
+        product = g.astype(F32) * o_ref[:, lanes].astype(F32)
+        delta = lax.dot_general(
+            ones, product, (((1,), (1,)), ((), ())), precision=EXACT, preferred_element_type=F32
+        )
+        prob = jnp.exp(dot(keys, q, 1, 1) * SCALE - norm_ref[head])
+        prob = jnp.where(j_row <= i_row, prob, 0.0)
+        sgrad = prob * (dot(values, g, 1, 1) - delta[0:1, :])
+        gv = gv + dot(prob.astype(BF16), g, 1, 0)
+        gk = gk + dot(sgrad.astype(BF16), q, 1, 0)
+        q_own, g_own = q_ref[own, lanes], g_ref[own, lanes]
+        g_own = jnp.where(live_own, g_own, zero)
+        product = g_own.astype(F32) * o_ref[own, lanes].astype(F32)
+        delta_own = jnp.sum(product, axis=1, keepdims=True)
+        norm_own = jnp.sum(jnp.where(diagonal, norm_ref[head], 0.0), axis=1, keepdims=True)
+        prob = jnp.exp(dot(q_own, all_keys, 1, 1) * SCALE - norm_own)
+        i_own = lax.broadcasted_iota(jnp.int32, prob.shape, 0) + p * 32
+        prob = jnp.where(position <= i_own, prob, 0.0)
+        sgrad = prob * (dot(g_own, all_values, 1, 1) - delta_own)
+        gq_ref[:, lanes] = dot(sgrad.astype(BF16), all_keys, 1, 0) * SCALE
+    gk_ref[...] = (gk * SCALE).astype(BF16)
+    gv_ref[...] = gv.astype(BF16)
 
 
 def shards(
@@ -404,7 +402,13 @@
         g,
         norms,
         *kv,
-        in_specs=[smem] * 2 + [vmem] * 8,
+        grid=(2,),
+        in_specs=[smem] * 2
+        + [pl.BlockSpec((slice_rows, STATS), lambda k: (0, k))] * 3
+        + [pl.BlockSpec((GROUP, 1, slice_rows), lambda k: (k, 0, 0))]
+        + [pl.BlockSpec((1280, HEAD_WIDTH), lambda k: (0, 0))] * 4,
+        out_specs=[pl.BlockSpec((own_rows, HEAD_WIDTH), lambda k: (0, k))] * 2
+        + [pl.BlockSpec((own_rows, STATS), lambda k: (0, k))],
         small=False,
     )
     parts = call(x_sum_kernel, [packed(256)] * 4, kv_grads[0], ahead, behind)

time: 118 us -> 118 us (level)
  no operation moved by 1% of the time
where the time goes in v4:
time: 118 us; the launch traced here: 116 us
  starting transfers between devices  45.1 us (38%)
  waiting for transfers between devices  43.7 us (37%)
  Pallas kernels  23.5 us (20%)
  other arithmetic  1.6 us (1%)
  between operations  1.54 us (1%)
    pallas_call x10, Pallas kernels, call(): pl.pallas_call(body, out_shape=out_shape, interpret=INTERPRET, compiler_p...  23.5 us
    all_to_all x3, starting transfers between devices, exchange(): return lax.all_to_all(tiles, axes, split_axis=0, concat_axis=0, tiled=True)  23.2 us
    ppermute x6, waiting for transfers between devices, shifted(): return lax.ppermute(value, ALONG_X, [(k, (k + by) % 4) for k in range(4)])  20.1 us
    all_to_all x3, waiting for transfers between devices, exchange(): return lax.all_to_all(tiles, axes, split_axis=0, concat_axis=0, tiled=True)  18.2 us
    ppermute x6, starting transfers between devices, shifted(): return lax.ppermute(value, ALONG_X, [(k, (k + by) % 4) for k in range(4)])  12.3 us
    ppermute x6, starting transfers between devices, crossed(): return lax.ppermute(value, ALONG_Y, [(k, k ^ by) for k in range(4)])  9.65 us
    ppermute x6, waiting for transfers between devices, crossed(): return lax.ppermute(value, ALONG_Y, [(k, k ^ by) for k in range(4)])  5.46 us
  transfers between devices with their start and end apart: 15, of which 7 were waited for; matrix products, arithmetic and copies ran while one was open for 2% of the time, Pallas kernels for 10%

profile of v4, /device:TPU:8, one launch (start us, length us, event | category | flops | bytes accessed | tf_op | source)
XLA Modules:
  0.0 116.3 jit_solution(4988210433370170315)
XLA Ops:
  1.3 3.0 %shard_map.128 = bf16[8,2,8,1024]{3,2,1,0:T(8,128)(2,1)} custom-call(s32[1]{0:T(128)} %bitcast.p_ref, s32[1]{0:T(128)} %bitcast.1.turn_ref, s32[1]{0:T(128)S(6)} %copy.17.live_ref, bf16[256,1792]{1,0:T(8,128)(2,1)} %bitcast.17, bf16[256,1792]{1,0:T(8,128)(2,1)} %bitcast.19, bf16[256,1792]{1,0:T(8,128)(2,1)} %bitcast.21, f32[14,1,256]{2,1,0:T(1,128)} %bitcast.26), custom_call_target="tpu_custom_call" | custom-call | tf_op jit(solution)/shard_map/pallas_call | solution.py:40
  4.3 0.0 copy-start.10
  4.3 10.4 %all-to-all-start = ((bf16[16,8,1024]{2,1,0:T(8,128)(2,1)}), bf16[16,8,1024]{2,1,0:T(8,128)(2,1)S(1)}, u32[]{:S(2)}, u32[]{:S(2)}) async-start(bf16[16,8,1024]{2,1,0:T(8,128)(2,1)} %bitcast.23), calls=%async_computation | async-start | bytes 524288 | tf_op jit(solution)/shard_map/all_to_all | solution.py:31
  14.9 3.5 %collective-permute-start.1 = (bf16[256,128]{1,0:T(8,128)(2,1)S(1)}, bf16[256,128]{1,0:T(8,128)(2,1)S(1)}, u32[]{:S(2)}, u32[]{:S(2)}) collective-permute-start(bf16[256,128]{1,0:T(8,128)(2,1)S(1)} %get-tuple-element.22), channel_id=1, source_target_pairs={{0,16},{2,18},{16,0},{18,2},{1,17},{3,19},{17,1},{19,3},{4,20},{6,... | collective-permute-start | bytes 196616 | tf_op jit(solution)/shard_map/ppermute | solution.py:240
  18.4 0.0 collective-permute-start.2
  18.4 1.3 %collective-permute-start = (bf16[384,128]{1,0:T(8,128)(2,1)S(1)}, bf16[384,128]{1,0:T(8,128)(2,1)S(1)}, u32[]{:S(2)}, u32[]{:S(2)}) collective-permute-start(bf16[384,128]{1,0:T(8,128)(2,1)S(1)} %get-tuple-element.21.own_ref), channel_id=1, source_target_pairs={{0,2},{2,0},{16,18},{18,16},{1,3},{3,1},{17,19},{19,17},{4,6},{6,4... | collective-permute-start | bytes 294920 | tf_op jit(solution)/shard_map/ppermute | solution.py:240
  19.8 1.5 %collective-permute-done.1.third_ref = bf16[256,128]{1,0:T(8,128)(2,1)S(1)} collective-permute-done((bf16[256,128]{1,0:T(8,128)(2,1)S(1)}, bf16[256,128]{1,0:T(8,128)(2,1)S(1)}, u32[]{:S(2)}, u32[]{:S(2)}) %collective-permute-start.1) | collective-permute-done | bytes 65568 | tf_op jit(solution)/shard_map/ppermute | solution.py:240
  21.3 2.0 %collective-permute-done.2.fourth_ref = bf16[256,128]{1,0:T(8,128)(2,1)S(1)} collective-permute-done((bf16[256,128]{1,0:T(8,128)(2,1)S(1)}, bf16[256,128]{1,0:T(8,128)(2,1)S(1)}, u32[]{:S(2)}, u32[]{:S(2)}) %collective-permute-start.2) | collective-permute-done | bytes 65568 | tf_op jit(solution)/shard_map/ppermute | solution.py:240
  23.3 1.9 %collective-permute-done.beside_ref = bf16[384,128]{1,0:T(8,128)(2,1)S(1)} collective-permute-done((bf16[384,128]{1,0:T(8,128)(2,1)S(1)}, bf16[384,128]{1,0:T(8,128)(2,1)S(1)}, u32[]{:S(2)}, u32[]{:S(2)}) %collective-permute-start) | collective-permute-done | bytes 98336 | tf_op jit(solution)/shard_map/ppermute | solution.py:240
  25.2 1.6 %collective-permute-start.3 = (bf16[1280,128]{1,0:T(8,128)(2,1)S(1)}, bf16[1280,128]{1,0:T(8,128)(2,1)S(1)}, u32[]{:S(2)}, u32[]{:S(2)}) collective-permute-start(bf16[1280,128]{1,0:T(8,128)(2,1)S(1)} %shard_map.131.refs_0_.kv0_ref), channel_id=1, source_target_pairs={{0,4},{4,8},{8,12},{12,0},{1,5},{5,9},{9,13},{13,1},{2,6},{6,10},{... | collective-permute-start | bytes 983048 | tf_op jit(solution)/shard_map/ppermute | solution.py:236
  26.8 2.7 %collective-permute-start.4 = (bf16[1280,128]{1,0:T(8,128)(2,1)S(1)}, bf16[1280,128]{1,0:T(8,128)(2,1)S(1)}, u32[]{:S(2)}, u32[]{:S(2)}) collective-permute-start(bf16[1280,128]{1,0:T(8,128)(2,1)S(1)} %shard_map.131.refs_0_.kv0_ref), channel_id=1, source_target_pairs={{0,8},{4,12},{8,0},{12,4},{1,9},{5,13},{9,1},{13,5},{2,10},{6,14},... | collective-permute-start | bytes 983048 | tf_op jit(solution)/shard_map/ppermute | solution.py:236
  29.5 1.4 %collective-permute-start.5 = (bf16[1280,128]{1,0:T(8,128)(2,1)S(1)}, bf16[1280,128]{1,0:T(8,128)(2,1)S(1)}, u32[]{:S(2)}, u32[]{:S(2)}) collective-permute-start(bf16[1280,128]{1,0:T(8,128)(2,1)S(1)} %shard_map.131.refs_0_.kv0_ref), channel_id=1, source_target_pairs={{0,12},{4,0},{8,4},{12,8},{1,13},{5,1},{9,5},{13,9},{2,14},{6,2},{... | collective-permute-start | bytes 983048 | tf_op jit(solution)/shard_map/ppermute | solution.py:236
  31.0 0.0 all-to-all-done.rows_ref
  31.0 1.4 %shard_map.129 = bf16[8,48,1024]{2,1,0:T(8,128)(2,1)} custom-call(s32[1]{0:T(128)} %bitcast.p_ref, s32[1]{0:T(128)} %bitcast.8.z_ref, bf16[16,8,1024]{2,1,0:T(8,128)(2,1)S(1)} %all-to-all-done.rows_ref), custom_call_target="tpu_custom_call" | custom-call | tf_op jit(solution)/shard_map/pallas_call | solution.py:40
  32.4 6.5 %all-to-all-start.1 = ((bf16[8,48,1024]{2,1,0:T(8,128)(2,1)}), bf16[8,48,1024]{2,1,0:T(8,128)(2,1)S(1)}, u32[]{:S(2)}, u32[]{:S(2)}) async-start(bf16[8,48,1024]{2,1,0:T(8,128)(2,1)} %shard_map.129), calls=%async_computation.1 | async-start | bytes 1572864 | tf_op jit(solution)/shard_map/all_to_all | solution.py:31
  38.9 0.4 fusion.5
  39.4 0.1 fusion.11
  39.5 0.1 select_reduce_fusion.2
  39.6 0.4 select_reduce_fusion.1
  40.0 0.1 select_reduce_fusion
  40.1 0.1 copy.15
  40.2 0.1 add_select_fusion
  40.3 0.1 copy.16
  40.4 0.1 iota_add_fusion
  40.5 0.1 broadcast_add_fusion
  40.6 0.1 iota_compare_fusion.3
  40.7 0.2 add.190.out_slot_ref
  40.9 0.1 add_select_fusion.2
  40.9 0.1 select_n.95.in_slot_ref
  41.0 0.0 collective-permute-done.3.refs_1_.kv1_ref
  41.1 1.8 %collective-permute-done.4.refs_2_.kv2_ref = bf16[1280,128]{1,0:T(8,128)(2,1)S(1)} collective-permute-done((bf16[1280,128]{1,0:T(8,128)(2,1)S(1)}, bf16[1280,128]{1,0:T(8,128)(2,1)S(1)}, u32[]{:S(2)}, u32[]{:S(2)}) %collective-permute-start.4) | collective-permute-done | bytes 327712 | tf_op jit(solution)/shard_map/ppermute | solution.py:236
  42.9 0.0 collective-permute-done.5.refs_3_.kv3_ref
  42.9 18.2 %all-to-all-done.1.rows_ref = bf16[8,48,1024]{2,1,0:T(8,128)(2,1)S(1)} async-done(((bf16[8,48,1024]{2,1,0:T(8,128)(2,1)}), bf16[8,48,1024]{2,1,0:T(8,128)(2,1)S(1)}, u32[]{:S(2)}, u32[]{:S(2)}) %all-to-all-start.1) | async-done | bytes 786464 | tf_op jit(solution)/shard_map/all_to_all | solution.py:31
  61.0 8.0 %shard_map.132 = (bf16[1024,128]{1,0:T(8,128)(2,1)}, bf16[1024,128]{1,0:T(8,128)(2,1)}, bf16[1024,128]{1,0:T(8,128)(2,1)}, bf16[1024,128]{1,0:T(8,128)(2,1)}, bf16[128,8,512]{2,1,0:T(8,128)(2,1)}) custom-call(s32[1,384]{1,0:T(1,128)S(1)} %select_n.95.in_slot_ref, s32[1,1024]{1,0:T(1,128)S(1)} %add.190.out_slot_ref, ...), custom_call_target="tpu_custom_call" | custom-call | tf_op jit(solution)/shard_map/pallas_call | solution.py:40
  69.0 6.3 %all-to-all-start.2 = ((bf16[128,8,512]{2,1,0:T(8,128)(2,1)}), bf16[128,8,512]{2,1,0:T(8,128)(2,1)S(1)}, u32[]{:S(2)}, u32[]{:S(2)}) async-start(bf16[128,8,512]{2,1,0:T(8,128)(2,1)} %get-tuple-element.23), calls=%async_computation.2 | async-start | bytes 2097152 | tf_op jit(solution)/shard_map/all_to_all | solution.py:31
  75.3 2.8 %collective-permute-start.7 = (bf16[1024,128]{1,0:T(8,128)(2,1)S(1)}, bf16[1024,128]{1,0:T(8,128)(2,1)S(1)}, u32[]{:S(2)}, u32[]{:S(2)}) collective-permute-start(bf16[1024,128]{1,0:T(8,128)(2,1)S(1)} %copy-done.12), channel_id=1, source_target_pairs={{0,12},{4,0},{8,4},{12,8},{1,13},{5,1},{9,5},{13,9},{2,14},{6,2},{... | collective-permute-start | bytes 786440 | tf_op jit(solution)/shard_map/ppermute | solution.py:236
  78.1 9.8 %collective-permute-done.7.relayed_ref = bf16[1024,128]{1,0:T(8,128)(2,1)S(1)} collective-permute-done((bf16[1024,128]{1,0:T(8,128)(2,1)S(1)}, bf16[1024,128]{1,0:T(8,128)(2,1)S(1)}, u32[]{:S(2)}, u32[]{:S(2)}) %collective-permute-start.7) | collective-permute-done | bytes 262176 | tf_op jit(solution)/shard_map/ppermute | solution.py:236
  88.0 0.1 shard_map.135
  88.0 3.7 %collective-permute-start.8 = (bf16[1024,128]{1,0:T(8,128)(2,1)S(1)}, bf16[1024,128]{1,0:T(8,128)(2,1)S(1)}, u32[]{:S(2)}, u32[]{:S(2)}) collective-permute-start(bf16[1024,128]{1,0:T(8,128)(2,1)S(1)} %shard_map.135), channel_id=1, source_target_pairs={{0,12},{4,0},{8,4},{12,8},{1,13},{5,1},{9,5},{13,9},{2,14},{6,2},{... | collective-permute-start | bytes 786440 | tf_op jit(solution)/shard_map/ppermute | solution.py:236
  91.8 8.4 %collective-permute-done.8.c_ref = bf16[1024,128]{1,0:T(8,128)(2,1)S(1)} collective-permute-done((bf16[1024,128]{1,0:T(8,128)(2,1)S(1)}, bf16[1024,128]{1,0:T(8,128)(2,1)S(1)}, u32[]{:S(2)}, u32[]{:S(2)}) %collective-permute-start.8) | collective-permute-done | bytes 262176 | tf_op jit(solution)/shard_map/ppermute | solution.py:236
  100.2 0.1 shard_map.136
  100.3 0.6 collective-permute-start.10
  100.9 1.7 %collective-permute-start.11 = (bf16[256,128]{1,0:T(8,128)(2,1)S(1)}, bf16[256,128]{1,0:T(8,128)(2,1)S(1)}, u32[]{:S(2)}, u32[]{:S(2)}) collective-permute-start(bf16[256,128]{1,0:T(8,128)(2,1)S(1)} %get-tuple-element.32), channel_id=1, source_target_pairs={{0,18},{2,16},{16,2},{18,0},{1,19},{3,17},{17,3},{19,1},{4,22},{6,... | collective-permute-start | bytes 196616 | tf_op jit(solution)/shard_map/ppermute | solution.py:240
  102.6 2.5 %collective-permute-start.9 = (bf16[256,128]{1,0:T(8,128)(2,1)S(1)}, bf16[256,128]{1,0:T(8,128)(2,1)S(1)}, u32[]{:S(2)}, u32[]{:S(2)}) collective-permute-start(bf16[256,128]{1,0:T(8,128)(2,1)S(1)} %get-tuple-element.30), channel_id=1, source_target_pairs={{0,2},{2,0},{16,18},{18,16},{1,3},{3,1},{17,19},{19,17},{4,6},{6,4... | collective-permute-start | bytes 196616 | tf_op jit(solution)/shard_map/ppermute | solution.py:240
  105.1 9.4 %shard_map.133 = (bf16[32,256]{1,0:T(8,128)(2,1)}, bf16[32,256]{1,0:T(8,128)(2,1)}, f32[32,1792]{1,0:T(8,128)}) custom-call(s32[1]{0:T(128)} %bitcast.p_ref, s32[1]{0:T(128)S(6)} %copy.17.live_ref, bf16[256,1792]{1,0:T(8,128)(2,1)} %bitcast.18, bf16[256,1792]{1,0:T(8,128)(2,1)} %bitcast.20, bf16[256,1792]{1,0:T(8,128)(2,1)} %bitcast.22, ...), custom_call_target="tpu_custom_call" | custom-call | tf_op jit(solution)/shard_map/pallas_call | solution.py:40
  114.5 0.7 shard_map.137
  115.2 0.3 copy-done.6
  115.5 0.8 shard_map.134
  (38 shorter events, 0.2 us)
Async XLA Ops:
  4.3 10.5 %copy-start.7 = (bf16[128,256]{1,0:T(8,128)(2,1)S(1)}, bf16[128,256]{1,0:T(8,128)(2,1)}, u32[]{:S(2)}) copy-start(bf16[128,256]{1,0:T(8,128)(2,1)} %pk_ref.1) | copy-start | bytes 196612
  4.3 10.5 %copy-start.8 = (bf16[128,256]{1,0:T(8,128)(2,1)S(1)}, bf16[128,256]{1,0:T(8,128)(2,1)}, u32[]{:S(2)}) copy-start(bf16[128,256]{1,0:T(8,128)(2,1)} %pv_ref.1) | copy-start | bytes 196612
  4.3 10.5 %copy-start.9 = (bf16[1,32,256]{2,1,0:T(8,128)(2,1)S(1)}, bf16[1,32,256]{2,1,0:T(8,128)(2,1)}, u32[]{:S(2)}) copy-start(bf16[1,32,256]{2,1,0:T(8,128)(2,1)} %param.16) | copy-start | bytes 49156
  4.3 10.5 %copy-start.10 = (bf16[1,32,256]{2,1,0:T(8,128)(2,1)S(1)}, bf16[1,32,256]{2,1,0:T(8,128)(2,1)}, u32[]{:S(2)}) copy-start(bf16[1,32,256]{2,1,0:T(8,128)(2,1)} %param.17) | copy-start | bytes 49156
  4.3 26.7 %all-to-all-start = ((bf16[16,8,1024]{2,1,0:T(8,128)(2,1)}), bf16[16,8,1024]{2,1,0:T(8,128)(2,1)S(1)}, u32[]{:S(2)}, u32[]{:S(2)}) async-start(bf16[16,8,1024]{2,1,0:T(8,128)(2,1)} %bitcast.23), calls=%async_computation | async-start | bytes 524288 | tf_op jit(solution)/shard_map/all_to_all | solution.py:31
  14.9 6.4 %collective-permute-start.1 = (bf16[256,128]{1,0:T(8,128)(2,1)S(1)}, bf16[256,128]{1,0:T(8,128)(2,1)S(1)}, u32[]{:S(2)}, u32[]{:S(2)}) collective-permute-start(bf16[256,128]{1,0:T(8,128)(2,1)S(1)} %get-tuple-element.22), channel_id=1, source_target_pairs={{0,16},{2,18},{16,0},{18,2},{1,17},{3,19},{17,1},{19,3},{4,20},{6,... | collective-permute-start | bytes 196616 | tf_op jit(solution)/shard_map/ppermute | solution.py:240
  18.4 5.0 %collective-permute-start.2 = (bf16[256,128]{1,0:T(8,128)(2,1)S(1)}, bf16[256,128]{1,0:T(8,128)(2,1)S(1)}, u32[]{:S(2)}, u32[]{:S(2)}) collective-permute-start(bf16[256,128]{1,0:T(8,128)(2,1)S(1)} %get-tuple-element.22), channel_id=1, source_target_pairs={{0,18},{2,16},{16,2},{18,0},{1,19},{3,17},{17,3},{19,1},{4,22},{6,... | collective-permute-start | bytes 196616 | tf_op jit(solution)/shard_map/ppermute | solution.py:240
  18.4 6.8 %collective-permute-start = (bf16[384,128]{1,0:T(8,128)(2,1)S(1)}, bf16[384,128]{1,0:T(8,128)(2,1)S(1)}, u32[]{:S(2)}, u32[]{:S(2)}) collective-permute-start(bf16[384,128]{1,0:T(8,128)(2,1)S(1)} %get-tuple-element.21.own_ref), channel_id=1, source_target_pairs={{0,2},{2,0},{16,18},{18,16},{1,3},{3,1},{17,19},{19,17},{4,6},{6,4... | collective-permute-start | bytes 294920 | tf_op jit(solution)/shard_map/ppermute | solution.py:240
  25.2 35.8 %copy-start = (bf16[1280,128]{1,0:T(8,128)(2,1)}, bf16[1280,128]{1,0:T(8,128)(2,1)S(1)}, u32[]{:S(2)}) copy-start(bf16[1280,128]{1,0:T(8,128)(2,1)S(1)} %shard_map.131.refs_0_.kv0_ref) | copy-start | bytes 983044
  25.2 15.8 %collective-permute-start.3 = (bf16[1280,128]{1,0:T(8,128)(2,1)S(1)}, bf16[1280,128]{1,0:T(8,128)(2,1)S(1)}, u32[]{:S(2)}, u32[]{:S(2)}) collective-permute-start(bf16[1280,128]{1,0:T(8,128)(2,1)S(1)} %shard_map.131.refs_0_.kv0_ref), channel_id=1, source_target_pairs={{0,4},{4,8},{8,12},{12,0},{1,5},{5,9},{9,13},{13,1},{2,6},{6,10},{... | collective-permute-start | bytes 983048 | tf_op jit(solution)/shard_map/ppermute | solution.py:236
  26.8 16.1 %collective-permute-start.4 = (bf16[1280,128]{1,0:T(8,128)(2,1)S(1)}, bf16[1280,128]{1,0:T(8,128)(2,1)S(1)}, u32[]{:S(2)}, u32[]{:S(2)}) collective-permute-start(bf16[1280,128]{1,0:T(8,128)(2,1)S(1)} %shard_map.131.refs_0_.kv0_ref), channel_id=1, source_target_pairs={{0,8},{4,12},{8,0},{12,4},{1,9},{5,13},{9,1},{13,5},{2,10},{6,14},... | collective-permute-start | bytes 983048 | tf_op jit(solution)/shard_map/ppermute | solution.py:236
  29.5 13.3 %collective-permute-start.5 = (bf16[1280,128]{1,0:T(8,128)(2,1)S(1)}, bf16[1280,128]{1,0:T(8,128)(2,1)S(1)}, u32[]{:S(2)}, u32[]{:S(2)}) collective-permute-start(bf16[1280,128]{1,0:T(8,128)(2,1)S(1)} %shard_map.131.refs_0_.kv0_ref), channel_id=1, source_target_pairs={{0,12},{4,0},{8,4},{12,8},{1,13},{5,1},{9,5},{13,9},{2,14},{6,2},{... | collective-permute-start | bytes 983048 | tf_op jit(solution)/shard_map/ppermute | solution.py:236
  32.4 28.6 %all-to-all-start.1 = ((bf16[8,48,1024]{2,1,0:T(8,128)(2,1)}), bf16[8,48,1024]{2,1,0:T(8,128)(2,1)S(1)}, u32[]{:S(2)}, u32[]{:S(2)}) async-start(bf16[8,48,1024]{2,1,0:T(8,128)(2,1)} %shard_map.129), calls=%async_computation.1 | async-start | bytes 1572864 | tf_op jit(solution)/shard_map/all_to_all | solution.py:31
  41.1 28.0 %copy-start.1 = (bf16[1280,128]{1,0:T(8,128)(2,1)}, bf16[1280,128]{1,0:T(8,128)(2,1)S(1)}, u32[]{:S(2)}) copy-start(bf16[1280,128]{1,0:T(8,128)(2,1)S(1)} %collective-permute-done.3.refs_1_.kv1_ref) | copy-start | bytes 983044
  42.9 26.1 %copy-start.2 = (bf16[1280,128]{1,0:T(8,128)(2,1)}, bf16[1280,128]{1,0:T(8,128)(2,1)S(1)}, u32[]{:S(2)}) copy-start(bf16[1280,128]{1,0:T(8,128)(2,1)S(1)} %collective-permute-done.4.refs_2_.kv2_ref) | copy-start | bytes 983044
  42.9 26.1 %copy-start.3 = (bf16[1280,128]{1,0:T(8,128)(2,1)}, bf16[1280,128]{1,0:T(8,128)(2,1)S(1)}, u32[]{:S(2)}) copy-start(bf16[1280,128]{1,0:T(8,128)(2,1)S(1)} %collective-permute-done.5.refs_3_.kv3_ref) | copy-start | bytes 983044
  69.0 6.3 %copy-start.12 = (bf16[1024,128]{1,0:T(8,128)(2,1)S(1)}, bf16[1024,128]{1,0:T(8,128)(2,1)}, u32[]{:S(2)}) copy-start(bf16[1024,128]{1,0:T(8,128)(2,1)} %get-tuple-element.28) | copy-start | bytes 786436
  69.0 9.1 %copy-start.11 = (bf16[1024,128]{1,0:T(8,128)(2,1)S(1)}, bf16[1024,128]{1,0:T(8,128)(2,1)}, u32[]{:S(2)}) copy-start(bf16[1024,128]{1,0:T(8,128)(2,1)} %get-tuple-element.26) | copy-start | bytes 786436
  69.0 18.9 %copy-start.5 = (bf16[1024,128]{1,0:T(8,128)(2,1)S(1)}, bf16[1024,128]{1,0:T(8,128)(2,1)}, u32[]{:S(2)}) copy-start(bf16[1024,128]{1,0:T(8,128)(2,1)} %get-tuple-element.27.own_ref) | copy-start | bytes 786436
  69.0 46.2 %all-to-all-start.2 = ((bf16[128,8,512]{2,1,0:T(8,128)(2,1)}), bf16[128,8,512]{2,1,0:T(8,128)(2,1)S(1)}, u32[]{:S(2)}, u32[]{:S(2)}) async-start(bf16[128,8,512]{2,1,0:T(8,128)(2,1)} %get-tuple-element.23), calls=%async_computation.2 | async-start | bytes 2097152 | tf_op jit(solution)/shard_map/all_to_all | solution.py:31
  75.3 12.6 %collective-permute-start.7 = (bf16[1024,128]{1,0:T(8,128)(2,1)S(1)}, bf16[1024,128]{1,0:T(8,128)(2,1)S(1)}, u32[]{:S(2)}, u32[]{:S(2)}) collective-permute-start(bf16[1024,128]{1,0:T(8,128)(2,1)S(1)} %copy-done.12), channel_id=1, source_target_pairs={{0,12},{4,0},{8,4},{12,8},{1,13},{5,1},{9,5},{13,9},{2,14},{6,2},{... | collective-permute-start | bytes 786440 | tf_op jit(solution)/shard_map/ppermute | solution.py:236
  78.1 13.6 %collective-permute-start.6 = (bf16[1024,128]{1,0:T(8,128)(2,1)S(1)}, bf16[1024,128]{1,0:T(8,128)(2,1)S(1)}, u32[]{:S(2)}, u32[]{:S(2)}) collective-permute-start(bf16[1024,128]{1,0:T(8,128)(2,1)S(1)} %copy-done.11), channel_id=1, source_target_pairs={{0,4},{4,8},{8,12},{12,0},{1,5},{5,9},{9,13},{13,1},{2,6},{6,10},{... | collective-permute-start | bytes 786440 | tf_op jit(solution)/shard_map/ppermute | solution.py:236
  88.0 12.2 %copy-start.4 = (bf16[1024,128]{1,0:T(8,128)(2,1)S(1)}, bf16[1024,128]{1,0:T(8,128)(2,1)}, u32[]{:S(2)}) copy-start(bf16[1024,128]{1,0:T(8,128)(2,1)} %get-tuple-element.25.a_ref) | copy-start | bytes 786436
  88.0 12.2 %collective-permute-start.8 = (bf16[1024,128]{1,0:T(8,128)(2,1)S(1)}, bf16[1024,128]{1,0:T(8,128)(2,1)S(1)}, u32[]{:S(2)}, u32[]{:S(2)}) collective-permute-start(bf16[1024,128]{1,0:T(8,128)(2,1)S(1)} %shard_map.135), channel_id=1, source_target_pairs={{0,12},{4,0},{8,4},{12,8},{1,13},{5,1},{9,5},{13,9},{2,14},{6,2},{... | collective-permute-start | bytes 786440 | tf_op jit(solution)/shard_map/ppermute | solution.py:236
  100.3 14.2 %collective-permute-start.10 = (bf16[256,128]{1,0:T(8,128)(2,1)S(1)}, bf16[256,128]{1,0:T(8,128)(2,1)S(1)}, u32[]{:S(2)}, u32[]{:S(2)}) collective-permute-start(bf16[256,128]{1,0:T(8,128)(2,1)S(1)} %get-tuple-element.31), channel_id=1, source_target_pairs={{0,16},{2,18},{16,0},{18,2},{1,17},{3,19},{17,1},{19,3},{4,20},{6,... | collective-permute-start | bytes 196616 | tf_op jit(solution)/shard_map/ppermute | solution.py:240
  100.9 13.6 %collective-permute-start.11 = (bf16[256,128]{1,0:T(8,128)(2,1)S(1)}, bf16[256,128]{1,0:T(8,128)(2,1)S(1)}, u32[]{:S(2)}, u32[]{:S(2)}) collective-permute-start(bf16[256,128]{1,0:T(8,128)(2,1)S(1)} %get-tuple-element.32), channel_id=1, source_target_pairs={{0,18},{2,16},{16,2},{18,0},{1,19},{3,17},{17,3},{19,1},{4,22},{6,... | collective-permute-start | bytes 196616 | tf_op jit(solution)/shard_map/ppermute | solution.py:240
  102.6 11.9 %collective-permute-start.9 = (bf16[256,128]{1,0:T(8,128)(2,1)S(1)}, bf16[256,128]{1,0:T(8,128)(2,1)S(1)}, u32[]{:S(2)}, u32[]{:S(2)}) collective-permute-start(bf16[256,128]{1,0:T(8,128)(2,1)S(1)} %get-tuple-element.30), channel_id=1, source_target_pairs={{0,2},{2,0},{16,18},{18,16},{1,3},{3,1},{17,19},{19,17},{4,6},{6,4... | collective-permute-start | bytes 196616 | tf_op jit(solution)/shard_map/ppermute | solution.py:240
  114.5 1.0 copy-start.6
